TPU v7x, 128 devices: a whole 4x4x4 slice. The times are simulated.
128 devices in a mesh: row: 8 (over z, core), col: 16 (over y, x).
Axes of the slice: x: 4, y: 4, z: 4, core: 2. Of those that a mesh axis runs over, the one named last changes fastest.
Arguments:
- a_matrix: float32 [8192, 8192], P('row', 'col'), may hold values from -14 to 30, as said below
- b_matrix: float32 [4096, 4096], P('row', 'col'), may hold values from -14 to 30, as said below
- c_matrix: float32 [8192, 4096], P('row', 'col'), may hold values from -6 to 6
Outputs:
- a_swept: float32 [8192, 8192], P('row', 'col')
- c_swept: float32 [8192, 4096], P('row', 'col')
- b_next: float32 [4096, 4096], P('row', 'col')
Inputs may be any that keep to these rules, and one draw needn't show every extreme that they name: `a_matrix`: symmetric positive definite; its smallest eigenvalue is at least 1. `b_matrix`: symmetric positive definite; its smallest eigenvalue is at least 1.
All inputs are finite; a program needn't handle non-finite values. Where the computation divides by a largest or mean magnitude, that divisor is 1e-20 or more.
Results may differ from a plain program's by a relative error of at most 0.00012.
Values sent between devices are 32-bit elements; how exact they have to be, the bound alone decides.
A program may use at most 128 MiB of HBM per device.

v0:
```python
import functools

import jax
import jax.numpy as jnp
from jax import lax
from jax.sharding import Mesh
from jax.sharding import PartitionSpec as P

PANEL = 256
PIVOT_ITERS = 6
STEPS_A = 2
STEPS_B = 16
ROW = ("row_0", "row_1")
COL = ("col_0", "col_1")
ROW_COL = ("row_0", "row_1", "col_0", "col_1")


EXACT = lax.Precision.HIGHEST


def spread(value, axis, source):
    kept = jnp.where(lax.axis_index(axis) == source, value, 0).astype(value.dtype)
    return lax.psum(kept, axis)


def from_root(shard, axis, root):
    return lax.dynamic_index_in_dim(lax.all_gather(shard, axis), root, 0, keepdims=False)


def over_axes(shard, axes):
    return functools.reduce(lax.psum, axes, shard)


def pivot_inverse(pivot):
    order = pivot.shape[0]
    scaling = 1.0 / jnp.sqrt(jnp.diagonal(pivot))
    unit = pivot * scaling[:, None] * scaling[None, :]
    ceiling = jnp.max(jnp.sum(jnp.abs(unit), axis=1))
    approx = jnp.eye(order, dtype=jnp.float32) / ceiling
    for turn in range(PIVOT_ITERS):
        product = jnp.dot(unit, approx, precision=EXACT, preferred_element_type=jnp.float32)
        approx = 2.0 * approx - jnp.dot(
            approx, product, precision=EXACT, preferred_element_type=jnp.float32
        )
    return approx * scaling[:, None] * scaling[None, :]


def frame(matrix, first):
    local_rows = matrix.shape[0]
    row_place = lax.axis_index(ROW)
    col_place = lax.axis_index(COL)
    global_rows = row_place * local_rows + jnp.arange(local_rows, dtype=jnp.int32)
    eye_rows = (global_rows[:, None] == first + jnp.arange(PANEL, dtype=jnp.int32)[None, :]).astype(
        jnp.float32
    )
    return (eye_rows, col_place)


def finish(matrix, solved, rows, first, eye_rows, col_place):
    local_cols = matrix.shape[1]
    offset = first % local_cols
    root_col = first // local_cols
    updated = matrix - jnp.dot(solved, rows, precision=EXACT, preferred_element_type=jnp.float32)
    current = updated[:, offset : offset + PANEL]
    placed = jnp.where(col_place == root_col, eye_rows - solved, current)
    return updated.at[:, offset : offset + PANEL].set(placed)


def a_step(matrix, other, step):
    local_rows, local_cols = matrix.shape
    other_cols = other.shape[1]
    first = step * PANEL
    root_row = first // local_rows
    row_offset = first % local_rows
    root_col = first // local_cols
    col_offset = first % local_cols
    eye_rows, col_place = frame(matrix, first)
    rows = matrix[row_offset : row_offset + PANEL, :]
    other_rows = other[row_offset : row_offset + PANEL, :]
    column = spread(matrix[:, col_offset : col_offset + PANEL], COL, root_col)
    pivot = column[row_offset : row_offset + PANEL, :]
    joined = from_root(jnp.concatenate([rows, other_rows, pivot], 1), ROW, root_row)
    rows = joined[:, :local_cols]
    other_rows = joined[:, local_cols : local_cols + other_cols]
    pivot = joined[:, local_cols + other_cols :]
    solved = jnp.dot(
        column - eye_rows, pivot_inverse(pivot), precision=EXACT, preferred_element_type=jnp.float32
    )
    new_matrix = finish(matrix, solved, rows, first, eye_rows, col_place)
    new_other = other - jnp.dot(
        solved, other_rows, precision=EXACT, preferred_element_type=jnp.float32
    )
    return (new_matrix, new_other)


def b_step(matrix, step):
    local_rows, local_cols = matrix.shape
    first = step * PANEL
    root_row = first // local_rows
    row_offset = first % local_rows
    root_col = first // local_cols
    eye_rows, col_place = frame(matrix, first)
    rows = from_root(matrix[row_offset : row_offset + PANEL, :], ROW, root_row)
    column = matrix - eye_rows
    here = jnp.dot(column, pivot_inverse(rows), precision=EXACT, preferred_element_type=jnp.float32)
    solved = from_root(here, COL, root_col)
    return finish(matrix, solved, rows, first, eye_rows, col_place)


def body(a_matrix, b_matrix, c_matrix):
    b_local = jnp.sum(b_matrix * b_matrix)
    b_squares = over_axes(b_local, ROW_COL)
    a_swept, c_swept = (a_matrix, c_matrix)
    for step in range(STEPS_A):
        a_swept, c_swept = a_step(a_swept, c_swept, step)
    b_inverse = b_matrix
    for step in range(STEPS_B):
        b_inverse = b_step(b_inverse, step)
    inv_local = jnp.sum(b_inverse * b_inverse)
    inv_squares = over_axes(inv_local, ROW_COL)
    scale = jnp.sqrt(jnp.sqrt(inv_squares / b_squares))
    b_next = 0.5 * (scale * b_matrix + b_inverse / scale)
    return (a_swept, c_swept, b_next)


def solution(mesh):
    finer = Mesh(mesh.devices.reshape(4, 2, 4, 4), ("row_0", "row_1", "col_0", "col_1"))
    placed = (P(ROW, COL), P(ROW, COL), P(ROW, COL))
    return jax.shard_map(
        body,
        mesh=finer,
        in_specs=placed,
        out_specs=(P(ROW, COL), P(ROW, COL), P(ROW, COL)),
        check_vma=False,
    )
```

profile of v0, /device:TPU:1, one launch (start us, length us, event | category | flops | bytes accessed | tf_op | source)
XLA Modules:
  0.0 2112.4 jit_solution(9269731013335773713)
XLA Ops:
  9.0 30.4 %all-gather.73.cloned.1.call-done = f32[2048,256]{1,0:T(8,128)} async-done(((f32[256,256]{1,0:T(8,128)}), f32[2048,256]{1,0:T(8,128)}) %all-gather.73.cloned.1.call-update) | async-done | bytes 2097168 | tf_op jit(solution)/shard_map/all_gather | solution.py:27
  52.7 70.4 %all-gather.75.cloned.1.call-done = f32[8192,256]{1,0:T(8,128)} async-done(((f32[512,256]{1,0:T(8,128)}), f32[8192,256]{1,0:T(8,128)}) %all-gather.75.cloned.1.call-update) | async-done | bytes 8388624 | tf_op jit(solution)/shard_map/all_gather | solution.py:27
  164.9 70.4 %all-gather.79.cloned.1.call-done = f32[8192,256]{1,0:T(8,128)} async-done(((f32[512,256]{1,0:T(8,128)}), f32[8192,256]{1,0:T(8,128)}) %all-gather.79.cloned.1.call-update) | async-done | bytes 8388624 | tf_op jit(solution)/shard_map/all_gather | solution.py:27
  238.0 25.9 %all-gather.81.cloned.1.call-done = f32[2048,256]{1,0:T(8,128)} async-done(((f32[256,256]{1,0:T(8,128)}), f32[2048,256]{1,0:T(8,128)}) %all-gather.81.cloned.1.call-update) | async-done | bytes 2097168 | tf_op jit(solution)/shard_map/all_gather | solution.py:27
  277.4 70.3 %all-gather.83.cloned.1.call-done = f32[8192,256]{1,0:T(8,128)} async-done(((f32[512,256]{1,0:T(8,128)}), f32[8192,256]{1,0:T(8,128)}) %all-gather.83.cloned.1.call-update) | async-done | bytes 8388624 | tf_op jit(solution)/shard_map/all_gather | solution.py:27
  350.3 25.9 %all-gather.85.cloned.1.call-done = f32[2048,256]{1,0:T(8,128)} async-done(((f32[256,256]{1,0:T(8,128)}), f32[2048,256]{1,0:T(8,128)}) %all-gather.85.cloned.1.call-update) | async-done | bytes 2097168 | tf_op jit(solution)/shard_map/all_gather | solution.py:27
  389.4 70.4 %all-gather.87.cloned.1.call-done = f32[8192,256]{1,0:T(8,128)} async-done(((f32[512,256]{1,0:T(8,128)}), f32[8192,256]{1,0:T(8,128)}) %all-gather.87.cloned.1.call-update) | async-done | bytes 8388624 | tf_op jit(solution)/shard_map/all_gather | solution.py:27
  462.7 25.7 %all-gather.89.cloned.1.call-done = f32[2048,256]{1,0:T(8,128)} async-done(((f32[256,256]{1,0:T(8,128)}), f32[2048,256]{1,0:T(8,128)}) %all-gather.89.cloned.1.call-update) | async-done | bytes 2097168 | tf_op jit(solution)/shard_map/all_gather | solution.py:27
  501.6 70.4 %all-gather.91.cloned.1.call-done = f32[8192,256]{1,0:T(8,128)} async-done(((f32[512,256]{1,0:T(8,128)}), f32[8192,256]{1,0:T(8,128)}) %all-gather.91.cloned.1.call-update) | async-done | bytes 8388624 | tf_op jit(solution)/shard_map/all_gather | solution.py:27
  574.7 25.9 %all-gather.93.cloned.1.call-done = f32[2048,256]{1,0:T(8,128)} async-done(((f32[256,256]{1,0:T(8,128)}), f32[2048,256]{1,0:T(8,128)}) %all-gather.93.cloned.1.call-update) | async-done | bytes 2097168 | tf_op jit(solution)/shard_map/all_gather | solution.py:27
  614.3 70.0 %all-gather.95.cloned.1.call-done = f32[8192,256]{1,0:T(8,128)} async-done(((f32[512,256]{1,0:T(8,128)}), f32[8192,256]{1,0:T(8,128)}) %all-gather.95.cloned.1.call-update) | async-done | bytes 8388624 | tf_op jit(solution)/shard_map/all_gather | solution.py:27
  687.0 25.9 %all-gather.97.cloned.1.call-done = f32[2048,256]{1,0:T(8,128)} async-done(((f32[256,256]{1,0:T(8,128)}), f32[2048,256]{1,0:T(8,128)}) %all-gather.97.cloned.1.call-update) | async-done | bytes 2097168 | tf_op jit(solution)/shard_map/all_gather | solution.py:27
  726.2 70.4 %all-gather.99.cloned.1.call-done = f32[8192,256]{1,0:T(8,128)} async-done(((f32[512,256]{1,0:T(8,128)}), f32[8192,256]{1,0:T(8,128)}) %all-gather.99.cloned.1.call-update) | async-done | bytes 8388624 | tf_op jit(solution)/shard_map/all_gather | solution.py:27
  799.4 25.7 %all-gather.101.cloned.1.call-done = f32[2048,256]{1,0:T(8,128)} async-done(((f32[256,256]{1,0:T(8,128)}), f32[2048,256]{1,0:T(8,128)}) %all-gather.101.cloned.1.call-update) | async-done | bytes 2097168 | tf_op jit(solution)/shard_map/all_gather | solution.py:27
  838.4 70.4 %all-gather.103.cloned.1.call-done = f32[8192,256]{1,0:T(8,128)} async-done(((f32[512,256]{1,0:T(8,128)}), f32[8192,256]{1,0:T(8,128)}) %all-gather.103.cloned.1.call-update) | async-done | bytes 8388624 | tf_op jit(solution)/shard_map/all_gather | solution.py:27
  911.4 25.9 %all-gather.105.cloned.1.call-done = f32[2048,256]{1,0:T(8,128)} async-done(((f32[256,256]{1,0:T(8,128)}), f32[2048,256]{1,0:T(8,128)}) %all-gather.105.cloned.1.call-update) | async-done | bytes 2097168 | tf_op jit(solution)/shard_map/all_gather | solution.py:27
  950.8 70.2 %all-gather.107.cloned.1.call-done = f32[8192,256]{1,0:T(8,128)} async-done(((f32[512,256]{1,0:T(8,128)}), f32[8192,256]{1,0:T(8,128)}) %all-gather.107.cloned.1.call-update) | async-done | bytes 8388624 | tf_op jit(solution)/shard_map/all_gather | solution.py:27
  1023.6 25.9 %all-gather.109.cloned.1.call-done = f32[2048,256]{1,0:T(8,128)} async-done(((f32[256,256]{1,0:T(8,128)}), f32[2048,256]{1,0:T(8,128)}) %all-gather.109.cloned.1.call-update) | async-done | bytes 2097168 | tf_op jit(solution)/shard_map/all_gather | solution.py:27
  1062.8 70.4 %all-gather.111.cloned.1.call-done = f32[8192,256]{1,0:T(8,128)} async-done(((f32[512,256]{1,0:T(8,128)}), f32[8192,256]{1,0:T(8,128)}) %all-gather.111.cloned.1.call-update) | async-done | bytes 8388624 | tf_op jit(solution)/shard_map/all_gather | solution.py:27
  1175.0 70.4 %all-gather.115.cloned.1.call-done = f32[8192,256]{1,0:T(8,128)} async-done(((f32[512,256]{1,0:T(8,128)}), f32[8192,256]{1,0:T(8,128)}) %all-gather.115.cloned.1.call-update) | async-done | bytes 8388624 | tf_op jit(solution)/shard_map/all_gather | solution.py:27
  1248.2 25.9 %all-gather.117.cloned.1.call-done = f32[2048,256]{1,0:T(8,128)} async-done(((f32[256,256]{1,0:T(8,128)}), f32[2048,256]{1,0:T(8,128)}) %all-gather.117.cloned.1.call-update) | async-done | bytes 2097168 | tf_op jit(solution)/shard_map/all_gather | solution.py:27
  1287.5 70.3 %all-gather.119.cloned.1.call-done = f32[8192,256]{1,0:T(8,128)} async-done(((f32[512,256]{1,0:T(8,128)}), f32[8192,256]{1,0:T(8,128)}) %all-gather.119.cloned.1.call-update) | async-done | bytes 8388624 | tf_op jit(solution)/shard_map/all_gather | solution.py:27
  1360.4 25.9 %all-gather.121.cloned.1.call-done = f32[2048,256]{1,0:T(8,128)} async-done(((f32[256,256]{1,0:T(8,128)}), f32[2048,256]{1,0:T(8,128)}) %all-gather.121.cloned.1.call-update) | async-done | bytes 2097168 | tf_op jit(solution)/shard_map/all_gather | solution.py:27
  1399.6 70.4 %all-gather.123.cloned.1.call-done = f32[8192,256]{1,0:T(8,128)} async-done(((f32[512,256]{1,0:T(8,128)}), f32[8192,256]{1,0:T(8,128)}) %all-gather.123.cloned.1.call-update) | async-done | bytes 8388624 | tf_op jit(solution)/shard_map/all_gather | solution.py:27
  1514.2 69.2 %all-gather.127.cloned.1.call-done = f32[8192,256]{1,0:T(8,128)} async-done(((f32[512,256]{1,0:T(8,128)}), f32[8192,256]{1,0:T(8,128)}) %all-gather.127.cloned.1.call-update) | async-done | bytes 8388624 | tf_op jit(solution)/shard_map/all_gather | solution.py:27
  1586.3 86.5 %all-reduce.7.cloned.1.call-done = f32[1024,256]{1,0:T(8,128)} async-done(((f32[1024,256]{1,0:T(8,128)}), f32[1024,256]{1,0:T(8,128)}) %all-reduce.7.cloned.1.call-update) | async-done | bytes 1048592 | tf_op jit(solution)/shard_map/psum | solution.py:23
  1674.9 26.7 %all-gather.129.cloned.1.call-done = f32[2048,256]{1,0:T(8,128)} async-done(((f32[256,256]{1,0:T(8,128)}), f32[2048,256]{1,0:T(8,128)}) %all-gather.129.cloned.1.call-update) | async-done | bytes 2097168 | tf_op jit(solution)/shard_map/all_gather | solution.py:27
  1716.0 38.0 %all-gather.69.cloned.1.call-done = f32[2048,1024]{1,0:T(8,128)} async-done(((f32[256,1024]{1,0:T(8,128)}), f32[2048,1024]{1,0:T(8,128)}) %all-gather.69.cloned.1.call-update) | async-done | bytes 8388624 | tf_op jit(solution)/shard_map/all_gather | solution.py:27
  1779.2 47.9 %all-gather.131.cloned.1.call-done = f32[8192,256]{1,0:T(8,128)} async-done(((f32[512,256]{1,0:T(8,128)}), f32[8192,256]{1,0:T(8,128)}) %all-gather.131.cloned.1.call-update) | async-done | bytes 8388624 | tf_op jit(solution)/shard_map/all_gather | solution.py:27
  1835.8 80.5 %all-reduce.9.cloned.1.call-done = f32[1024,256]{1,0:T(8,128)} async-done(((f32[1024,256]{1,0:T(8,128)}), f32[1024,256]{1,0:T(8,128)}) %all-reduce.9.cloned.1.call-update) | async-done | bytes 1048592 | tf_op jit(solution)/shard_map/psum | solution.py:23
  1959.7 37.5 %all-gather.71.cloned.1.call-done = f32[2048,1024]{1,0:T(8,128)} async-done(((f32[256,1024]{1,0:T(8,128)}), f32[2048,1024]{1,0:T(8,128)}) %all-gather.71.cloned.1.call-update) | async-done | bytes 8388624 | tf_op jit(solution)/shard_map/all_gather | solution.py:27
  2024.3 45.6 %all-gather.135.cloned.1.call-done = f32[8192,256]{1,0:T(8,128)} async-done(((f32[512,256]{1,0:T(8,128)}), f32[8192,256]{1,0:T(8,128)}) %all-gather.135.cloned.1.call-update) | async-done | bytes 8388624 | tf_op jit(solution)/shard_map/all_gather | solution.py:27
  (529 shorter events, 446.1 us)
Async XLA Ops:
  8.9 114.2 %all-gather.75.cloned.1.call-start = ((), (), s32[]{:S(2)}) async-start(), calls=%async_computation.5 | async-start | bytes 8912896 | tf_op jit(solution)/shard_map/all_gather | solution.py:27
  52.7 99.0 %all-gather.77.cloned.1.call-start = ((), (), s32[]{:S(2)}) async-start(), calls=%async_computation.6 | async-start | bytes 2359296 | tf_op jit(solution)/shard_map/all_gather | solution.py:27
  125.7 109.7 %all-gather.79.cloned.1.call-start = ((), (), s32[]{:S(2)}) async-start(), calls=%async_computation.7 | async-start | bytes 8912896 | tf_op jit(solution)/shard_map/all_gather | solution.py:27
  164.9 99.1 %all-gather.81.cloned.1.call-start = ((), (), s32[]{:S(2)}) async-start(), calls=%async_computation.8 | async-start | bytes 2359296 | tf_op jit(solution)/shard_map/all_gather | solution.py:27
  238.0 109.7 %all-gather.83.cloned.1.call-start = ((), (), s32[]{:S(2)}) async-start(), calls=%async_computation.9 | async-start | bytes 8912896 | tf_op jit(solution)/shard_map/all_gather | solution.py:27
  277.2 99.0 %all-gather.85.cloned.1.call-start = ((), (), s32[]{:S(2)}) async-start(), calls=%async_computation.10 | async-start | bytes 2359296 | tf_op jit(solution)/shard_map/all_gather | solution.py:27
  350.2 109.6 %all-gather.87.cloned.1.call-start = ((), (), s32[]{:S(2)}) async-start(), calls=%async_computation.11 | async-start | bytes 8912896 | tf_op jit(solution)/shard_map/all_gather | solution.py:27
  462.4 109.7 %all-gather.91.cloned.1.call-start = ((), (), s32[]{:S(2)}) async-start(), calls=%async_computation.13 | async-start | bytes 8912896 | tf_op jit(solution)/shard_map/all_gather | solution.py:27
  501.6 99.0 %all-gather.93.cloned.1.call-start = ((), (), s32[]{:S(2)}) async-start(), calls=%async_computation.14 | async-start | bytes 2359296 | tf_op jit(solution)/shard_map/all_gather | solution.py:27
  574.6 109.6 %all-gather.95.cloned.1.call-start = ((), (), s32[]{:S(2)}) async-start(), calls=%async_computation.15 | async-start | bytes 8912896 | tf_op jit(solution)/shard_map/all_gather | solution.py:27
  613.8 99.0 %all-gather.97.cloned.1.call-start = ((), (), s32[]{:S(2)}) async-start(), calls=%async_computation.16 | async-start | bytes 2359296 | tf_op jit(solution)/shard_map/all_gather | solution.py:27
  686.9 109.7 %all-gather.99.cloned.1.call-start = ((), (), s32[]{:S(2)}) async-start(), calls=%async_computation.17 | async-start | bytes 8912896 | tf_op jit(solution)/shard_map/all_gather | solution.py:27
  799.1 109.6 %all-gather.103.cloned.1.call-start = ((), (), s32[]{:S(2)}) async-start(), calls=%async_computation.19 | async-start | bytes 8912896 | tf_op jit(solution)/shard_map/all_gather | solution.py:27
  911.3 109.7 %all-gather.107.cloned.1.call-start = ((), (), s32[]{:S(2)}) async-start(), calls=%async_computation.21 | async-start | bytes 8912896 | tf_op jit(solution)/shard_map/all_gather | solution.py:27
  950.5 99.0 %all-gather.109.cloned.1.call-start = ((), (), s32[]{:S(2)}) async-start(), calls=%async_computation.22 | async-start | bytes 2359296 | tf_op jit(solution)/shard_map/all_gather | solution.py:27
  1023.6 109.6 %all-gather.111.cloned.1.call-start = ((), (), s32[]{:S(2)}) async-start(), calls=%async_computation.23 | async-start | bytes 8912896 | tf_op jit(solution)/shard_map/all_gather | solution.py:27
  1062.7 99.0 %all-gather.113.cloned.1.call-start = ((), (), s32[]{:S(2)}) async-start(), calls=%async_computation.24 | async-start | bytes 2359296 | tf_op jit(solution)/shard_map/all_gather | solution.py:27
  1135.8 109.7 %all-gather.115.cloned.1.call-start = ((), (), s32[]{:S(2)}) async-start(), calls=%async_computation.25 | async-start | bytes 8912896 | tf_op jit(solution)/shard_map/all_gather | solution.py:27
  1175.0 99.1 %all-gather.117.cloned.1.call-start = ((), (), s32[]{:S(2)}) async-start(), calls=%async_computation.26 | async-start | bytes 2359296 | tf_op jit(solution)/shard_map/all_gather | solution.py:27
  1248.1 109.7 %all-gather.119.cloned.1.call-start = ((), (), s32[]{:S(2)}) async-start(), calls=%async_computation.27 | async-start | bytes 8912896 | tf_op jit(solution)/shard_map/all_gather | solution.py:27
  1287.3 99.0 %all-gather.121.cloned.1.call-start = ((), (), s32[]{:S(2)}) async-start(), calls=%async_computation.28 | async-start | bytes 2359296 | tf_op jit(solution)/shard_map/all_gather | solution.py:27
  1360.4 109.7 %all-gather.123.cloned.1.call-start = ((), (), s32[]{:S(2)}) async-start(), calls=%async_computation.29 | async-start | bytes 8912896 | tf_op jit(solution)/shard_map/all_gather | solution.py:27
  1399.5 99.0 %all-gather.125.cloned.1.call-start = ((), (), s32[]{:S(2)}) async-start(), calls=%async_computation.30 | async-start | bytes 2359296 | tf_op jit(solution)/shard_map/all_gather | solution.py:27
  1472.6 110.8 %all-gather.127.cloned.1.call-start = ((), (), s32[]{:S(2)}) async-start(), calls=%async_computation.31 | async-start | bytes 8912896 | tf_op jit(solution)/shard_map/all_gather | solution.py:27
  1512.9 159.8 %all-reduce.7.cloned.1.call-start = ((), (), s32[]{:S(2)}) async-start(), calls=%async_computation | async-start | bytes 2097152 | tf_op jit(solution)/shard_map/psum | solution.py:23
  1514.1 187.5 %all-gather.129.cloned.1.call-start = ((), (), s32[]{:S(2)}) async-start(), calls=%async_computation.32 | async-start | bytes 2359296 | tf_op jit(solution)/shard_map/all_gather | solution.py:27
  1586.2 167.9 %all-gather.69.cloned.1.call-start = ((), (), s32[]{:S(2)}) async-start(), calls=%async_computation.2 | async-start | bytes 9437184 | tf_op jit(solution)/shard_map/all_gather | solution.py:27
  1674.8 152.2 %all-gather.131.cloned.1.call-start = ((), (), s32[]{:S(2)}) async-start(), calls=%async_computation.33 | async-start | bytes 8912896 | tf_op jit(solution)/shard_map/all_gather | solution.py:27
  1714.8 201.4 %all-reduce.9.cloned.1.call-start = ((), (), s32[]{:S(2)}) async-start(), calls=%async_computation.1 | async-start | bytes 2097152 | tf_op jit(solution)/shard_map/psum | solution.py:23
  1779.1 165.6 %all-gather.133.cloned.1.call-start = ((), (), s32[]{:S(2)}) async-start(), calls=%async_computation.34 | async-start | bytes 2359296 | tf_op jit(solution)/shard_map/all_gather | solution.py:27
  1830.7 166.5 %all-gather.71.cloned.1.call-start = ((), (), s32[]{:S(2)}) async-start(), calls=%async_computation.3 | async-start | bytes 9437184 | tf_op jit(solution)/shard_map/all_gather | solution.py:27
  1919.4 150.5 %all-gather.135.cloned.1.call-start = ((), (), s32[]{:S(2)}) async-start(), calls=%async_computation.35 | async-start | bytes 8912896 | tf_op jit(solution)/shard_map/all_gather | solution.py:27
  (32 other events, 762.4 us)
Sparse Core Ops, SparseCore 0:
  10.3 29.1 all-gather.72
  52.8 70.3 all-gather.74
  125.8 25.7 all-gather.76
  165.0 70.3 all-gather.78
  238.1 25.7 all-gather.80
  277.3 70.3 all-gather.82
  389.5 70.3 all-gather.86
  462.5 25.7 all-gather.88
  501.7 70.3 all-gather.90
  574.8 25.7 all-gather.92
  613.9 70.3 all-gather.94
  687.0 25.7 all-gather.96
  726.2 70.3 all-gather.98
  838.4 70.3 all-gather.102
  911.5 25.7 all-gather.104
  950.6 70.3 all-gather.106
  1062.9 70.3 all-gather.110
  1135.9 25.7 all-gather.112
  1175.1 70.3 all-gather.114
  1248.2 25.7 all-gather.116
  1287.4 70.3 all-gather.118
  1360.5 25.7 all-gather.120
  1399.7 70.3 all-gather.122
  1513.0 70.3 all-gather.126
  1587.2 85.4 all-reduce.6
  1674.9 26.6 all-gather.128
  1703.9 50.1 all-gather.68
  1756.8 70.2 all-gather.130
  1830.7 85.4 all-reduce.8
  1918.0 26.6 all-gather.132
  1947.0 50.1 all-gather.70
  1999.7 70.0 all-gather.134
  (4 shorter events, 102.9 us)
where the time goes:
time: 2120 us; the launch traced here: 2110 us
  waiting for transfers between devices  1740 us (82%)
  matrix products  185 us (9%)
  local copies, waits for them, and re-layouts  80.5 us (4%)
  other arithmetic  42.6 us (2%)
  blocking collectives  31.1 us (1%)
  between operations  31 us (1%)
    all_gather x34, waiting for transfers between devices, from_root(): lax.all_gather(shard, axis)  1570 us
    psum x2, waiting for transfers between devices, spread(): return lax.psum(kept, axis)  167 us
    dot_general x108, matrix products, pivot_inverse(): jnp.dot(unit, approx, precision=EXACT, preferred_element_type=jnp.float32)  74.2 us
  transfers between devices with their start and end apart: 36, of which 36 were waited for; matrix products, arithmetic and copies ran while one was open for 4% of the time, Pallas kernels for 0%

commit v1 on v0

v1 whole, which is shorter than its diff:
```python
import functools

import jax
import jax.numpy as jnp
from jax import lax
from jax.experimental import pallas as pl
from jax.experimental.pallas import tpu as pltpu
from jax.sharding import Mesh
from jax.sharding import PartitionSpec as P

PANEL = 256
SQUARINGS = 5
STEPS_A = 2
STEPS_B = 16
JOINED = 4
AXES = ("z", "core", "y", "x")
ROW = ("z", "core")
COL = ("y", "x")
F32 = jnp.float32
BF16 = jnp.bfloat16


def halves(value):
    high = value.astype(BF16)
    return high, (value - high.astype(F32)).astype(BF16)


def product(left, right):
    return jnp.dot(left, right, preferred_element_type=F32)


def triple(left, right_high, right_low):
    high, low = halves(left)
    return product(high, right_high) + product(high, right_low) + product(low, right_high)


def pivot_inverse(pivot):
    shape = (PANEL, PANEL)
    unit = lax.broadcasted_iota(jnp.int32, shape, 0) == lax.broadcasted_iota(jnp.int32, shape, 1)
    diagonal = jnp.where(unit, pivot, 0.0)
    down = 1.0 / jnp.sqrt(jnp.sum(diagonal, axis=1, keepdims=True))
    across = 1.0 / jnp.sqrt(jnp.sum(diagonal, axis=0, keepdims=True))
    scaled = pivot * down * across
    ceiling = jnp.max(jnp.sum(jnp.abs(scaled), axis=1, keepdims=True), axis=0, keepdims=True)
    eye = jnp.where(unit, 1.0, 0.0)
    power = eye - scaled / ceiling
    total = eye + power
    high, low = halves(power)
    power = product(high, high) + product(high, low) + product(low, high)
    for turn in range(SQUARINGS - 1):
        high, low = halves(jnp.concatenate([power, total], 0))
        both = product(high, high[:PANEL]) + product(high, low[:PANEL]) + product(low, high[:PANEL])
        power = both[:PANEL]
        total = total + both[PANEL:]
    high, low = halves(power)
    total = total + triple(total, high, low)
    return total / ceiling * down * across


def composite(count, table, fresh, fresh_high, fresh_low):
    @pl.loop(0, count)
    def _(p):
        here = pl.ds(pl.multiple_of(p * PANEL, PANEL), PANEL)
        inverse = pivot_inverse(table[here, here])
        high, low = halves(table[here, :])
        fresh[...] = triple(inverse, high, low)
        fresh[:, here] = inverse
        high, low = halves(fresh[...])
        fresh_high[...] = high
        fresh_low[...] = low

        @pl.loop(0, count)
        def _(q):
            @pl.when(q != p)
            def _():
                there = pl.ds(pl.multiple_of(q * PANEL, PANEL), PANEL)
                column = table[there, here]
                table[there, here] = jnp.zeros((PANEL, PANEL), F32)
                table[there, :] = table[there, :] - triple(column, fresh_high[...], fresh_low[...])

        table[here, :] = fresh[...]


def right_side(table, rows, base, right_high, right_low, solved_high, solved_low):
    order, cols = rows.shape
    if base is None:
        value = rows[...]
    else:
        unit = lax.broadcasted_iota(jnp.int32, (order, cols), 0) == base + lax.broadcasted_iota(jnp.int32, (order, cols), 1)
        inside = jnp.logical_and(base >= 0, base < order)
        value = jnp.where(inside, jnp.where(unit, 1.0, 0.0), rows[...])
    high, low = halves(value)
    right_high[:, :cols] = high
    right_low[:, :cols] = low

    @pl.loop(0, order // PANEL)
    def _(q):
        there = pl.ds(pl.multiple_of(q * PANEL, PANEL), PANEL)
        high, low = halves(triple(table[there, :], right_high[:, :cols], right_low[:, :cols]))
        solved_high[there, :cols] = high
        solved_low[there, :cols] = low


def left_side(matrix, result, piece, row_base, col_base, order, solved_high, solved_low):
    rows, cols = matrix.shape

    @pl.loop(0, rows // PANEL)
    def _(r):
        start = pl.multiple_of(r * PANEL, PANEL)
        there = pl.ds(start, PANEL)
        down = row_base + start + lax.broadcasted_iota(jnp.int32, (PANEL, PANEL), 0)
        total = None
        for q in range(order // PANEL):
            unit = down == q * PANEL + lax.broadcasted_iota(jnp.int32, (PANEL, PANEL), 1)
            column = piece(start, q) - jnp.where(unit, 1.0, 0.0)
            among = pl.ds(q * PANEL, PANEL)
            part = triple(column, solved_high[among, :cols], solved_low[among, :cols])
            total = part if total is None else total + part
        base = matrix[there, :]
        if col_base is not None:
            inside = jnp.logical_and(col_base >= 0, col_base < order)
            across = col_base + lax.broadcasted_iota(jnp.int32, (PANEL, cols), 1)
            begin = row_base + start + lax.broadcasted_iota(jnp.int32, (PANEL, cols), 0)
            base = jnp.where(inside, jnp.where(begin == across, 1.0, 0.0), base)
        result[there, :] = base - total


def center_kernel(step, mine, other, matrix, mate, half, table, fresh, fresh_high, fresh_low, right_high, right_low, solved_high, solved_low):
    core = lax.axis_index("core")
    rows = matrix.shape[0]
    order = JOINED * PANEL
    base = (lax.axis_index("y") - step) * order + lax.axis_index("x") * matrix.shape[1]

    @pl.when(lax.axis_index("z") == step)
    def _():
        ours = pl.ds(pl.multiple_of(core * rows, rows), rows)
        theirs = pl.ds(pl.multiple_of((1 - core) * rows, rows), rows)
        for q in range(JOINED):
            table[ours, q * PANEL : (q + 1) * PANEL] = mine[q]
            table[theirs, q * PANEL : (q + 1) * PANEL] = other[q]
        composite(JOINED, table, fresh, fresh_high, fresh_low)
        inside = jnp.logical_and(base >= 0, base < order)
        for there, source in ((ours, matrix), (theirs, mate)):
            shape = source.shape
            down = there.start + lax.broadcasted_iota(jnp.int32, shape, 0)
            unit = down == base + lax.broadcasted_iota(jnp.int32, shape, 1)
            high, low = halves(jnp.where(inside, jnp.where(unit, 1.0, 0.0), source[...]))
            right_high[there, :] = high
            right_low[there, :] = low
        for q in range(rows // PANEL):
            there = pl.ds(pl.multiple_of(core * rows + q * PANEL, PANEL), PANEL)
            half[q * PANEL : (q + 1) * PANEL, :] = triple(table[there, :], right_high[...], right_low[...])


def update_kernel(step, matrix, column, solved, result, solved_high, solved_low):
    order = JOINED * PANEL
    rows = matrix.shape[0]
    row_base = (lax.axis_index("z") - step) * order + lax.axis_index("core") * rows
    col_base = (lax.axis_index("y") - step) * order + lax.axis_index("x") * matrix.shape[1]
    for core in range(2):
        high, low = halves(solved[core])
        solved_high[core * rows : (core + 1) * rows, :] = high
        solved_low[core * rows : (core + 1) * rows, :] = low
    piece = lambda start, q: column[q, pl.ds(start, PANEL), :]
    left_side(matrix, result, piece, row_base, col_base, order, solved_high, solved_low)


def ring(index, by):
    return lax.rem(index + by, 4)


def send(source, target, sent, received, where):
    return pltpu.make_async_remote_copy(
        src_ref=source, dst_ref=target, send_sem=sent, recv_sem=received,
        device_id=where, device_id_type=pl.DeviceIdType.MESH,
    )


def greet(neighbours):
    barrier = pltpu.get_barrier_semaphore()
    for where in neighbours:
        pl.semaphore_signal(barrier, inc=1, device_id=where, device_id_type=pl.DeviceIdType.MESH)
    pl.semaphore_wait(barrier, len(neighbours))


def part(h):
    return pl.ds(h * PANEL, PANEL)


def spread(axis, step, source, landing, sent, received, follow):
    place = lax.axis_index(axis)
    apart = lax.rem(place - step + 4, 4)
    up, down = {axis: ring(place, 1)}, {axis: ring(place, 3)}
    outward = [send(source.at[part(h)], landing.at[part(h)], sent.at[0, h], received.at[h], up) for h in (0, 1)]
    inward = [send(source.at[part(h)], landing.at[part(h)], sent.at[1, h], received.at[h], down) for h in (0, 1)]
    onward = send(landing.at[part(0)], landing.at[part(0)], sent.at[0, 0], received.at[0], up)
    backward = send(landing.at[part(1)], landing.at[part(1)], sent.at[1, 1], received.at[1], down)

    @pl.when(apart == 0)
    def _():
        for copy in (outward[0], inward[1], outward[1], inward[0]):
            copy.start()
        follow(0, source)
        follow(1, source)

    def arrive(h):
        send(landing.at[part(h)], landing.at[part(h)], sent.at[0, h], received.at[h], up).wait_recv()

    @pl.when(apart == 1)
    def _():
        arrive(0)
        onward.start()
        follow(0, landing)
        arrive(1)
        follow(1, landing)

    @pl.when(apart == 3)
    def _():
        arrive(1)
        backward.start()
        follow(1, landing)
        arrive(0)
        follow(0, landing)

    @pl.when(apart == 2)
    def _():
        arrive(0)
        follow(0, landing)
        arrive(1)
        follow(1, landing)

    def finish():
        @pl.when(apart == 0)
        def _():
            for copy in outward + inward:
                copy.wait_send()

        @pl.when(apart == 1)
        def _():
            onward.wait_send()

        @pl.when(apart == 3)
        def _():
            backward.wait_send()

    return apart, finish


def gather_kernel(step, matrix, column, other, mate, y_sent, y_got, x_sent, x_got, far_sent, far_got, core_sent, core_got):
    x, y = lax.axis_index("x"), lax.axis_index("y")
    right, left, far = ring(x, 1), ring(x, 3), ring(x, 2)
    partner = {"core": 1 - lax.axis_index("core")}
    center = lax.axis_index("z") == step
    greet([{"y": ring(y, 1)}, {"y": ring(y, 3)}, {"x": right}, {"x": left}, partner])
    swap = send(matrix, mate, core_sent.at[4], core_got.at[4], partner)

    @pl.when(center)
    def _():
        swap.start()

    def sideways(h, ref):
        return [
            send(ref.at[part(h)], column.at[x, part(h)], x_sent.at[0, h], x_got.at[0, h], {"x": right}),
            send(ref.at[part(h)], column.at[x, part(h)], x_sent.at[1, h], x_got.at[1, h], {"x": left}),
        ]

    def follow(h, ref):
        for copy in sideways(h, ref):
            copy.start()

    apart, finish = spread("y", step, matrix, column.at[x], y_sent, y_got, follow)

    def give(role, place, ref):
        return send(ref, other.at[place], core_sent.at[role], core_got.at[role], partner)

    @pl.when(jnp.logical_and(center, apart == 0))
    def _():
        give(0, x, matrix).start()

    @pl.when(jnp.logical_and(center, apart != 0))
    def _():
        give(0, x, column.at[x]).start()

    @pl.when(apart == 0)
    def _():
        column[x] = matrix[...]

    def arrive(place, h, received):
        ref = column.at[place, part(h)]
        send(ref, ref, x_sent.at[0, h], received, {"x": right}).wait_recv()

    arrive(left, 0, x_got.at[0, 0])
    onward = send(column.at[left, part(0)], column.at[left, part(0)], far_sent.at[0], far_got.at[0], {"x": right})
    onward.start()
    arrive(right, 1, x_got.at[1, 1])
    backward = send(column.at[right, part(1)], column.at[right, part(1)], far_sent.at[1], far_got.at[1], {"x": left})
    backward.start()
    arrive(left, 1, x_got.at[0, 1])
    arrive(right, 0, x_got.at[1, 0])

    @pl.when(center)
    def _():
        give(1, left, column.at[left]).start()
        give(2, right, column.at[right]).start()

    arrive(far, 0, far_got.at[0])
    arrive(far, 1, far_got.at[1])

    @pl.when(center)
    def _():
        give(3, far, column.at[far]).start()

    finish()
    for h in (0, 1):
        for copy in sideways(h, matrix):
            copy.wait_send()
    onward.wait_send()
    backward.wait_send()

    @pl.when(center)
    def _():
        swap.wait()
        for role, place in enumerate((x, left, right, far)):
            give(role, place, column.at[place]).wait()


def share_kernel(step, half, solved, z_sent, z_got, core_sent, core_got):
    z, core = lax.axis_index("z"), lax.axis_index("core")
    partner = {"core": 1 - core}
    greet([{"z": ring(z, 1)}, {"z": ring(z, 3)}, partner])

    def give(h, ref):
        return send(ref.at[part(h)], solved.at[core, part(h)], core_sent.at[h], core_got.at[h], partner)

    def follow(h, ref):
        give(h, ref).start()

    apart, finish = spread("z", step, half, solved.at[core], z_sent, z_got, follow)

    @pl.when(apart == 0)
    def _():
        solved[core] = half[...]

    finish()
    for h in (0, 1):
        give(h, half).wait_send()
        ref = solved.at[1 - core, part(h)]
        send(ref, ref, core_sent.at[h], core_got.at[h], partner).wait_recv()


def sum_kernel(value, total, first, second, between, first_sent, first_got, second_sent, second_got):
    z, core, y, x = (lax.axis_index(axis) for axis in AXES)
    line, plane = z * 2 + core, y * 4 + x

    def of_line(by):
        place = lax.rem(line + by, 8)
        return {"z": place // 2, "core": lax.rem(place, 2)}

    def of_plane(by):
        place = lax.rem(plane + by, 16)
        return {"y": place // 4, "x": lax.rem(place, 4)}

    greet([of_line(by) for by in range(1, 8)] + [of_plane(by) for by in range(1, 16)])
    copies = [send(value, first.at[by - 1], first_sent.at[by - 1], first_got.at[by - 1], of_line(by)) for by in range(1, 8)]
    for copy in copies:
        copy.start()
    for copy in copies:
        copy.wait()
    result = value[...]
    for by in range(7):
        result = result + first[by]
    between[...] = result
    copies = [send(between, second.at[by - 1], second_sent.at[by - 1], second_got.at[by - 1], of_plane(by)) for by in range(1, 16)]
    for copy in copies:
        copy.start()
    for copy in copies:
        copy.wait()
    for by in range(15):
        result = result + second[by]
    total[...] = result


def a_kernel(matrix, other, column, row, other_row, pivot, result, other_result, table, fresh, fresh_high, fresh_low, right_high, right_low, solved_high, solved_low):
    order = STEPS_A * PANEL
    row_base = (lax.axis_index("z") * 2 + lax.axis_index("core")) * matrix.shape[0]
    col_base = (lax.axis_index("y") * 4 + lax.axis_index("x")) * matrix.shape[1]
    table[...] = pivot[...]
    composite(STEPS_A, table, fresh, fresh_high, fresh_low)

    def piece(start, q):
        among = pl.ds(pl.multiple_of(start % order, PANEL), PANEL)
        return column[start // order, pl.ds(q * PANEL, PANEL), among].T

    right_side(table, row, col_base, right_high, right_low, solved_high, solved_low)
    left_side(matrix, result, piece, row_base, col_base, order, solved_high, solved_low)
    right_side(table, other_row, None, right_high, right_low, solved_high, solved_low)
    left_side(other, other_result, piece, row_base, None, order, solved_high, solved_low)


def scratch(order, cols):
    return [
        pltpu.VMEM((order, order), F32),
        pltpu.VMEM((PANEL, order), F32),
        pltpu.VMEM((PANEL, order), BF16),
        pltpu.VMEM((PANEL, order), BF16),
        pltpu.VMEM((order, cols), BF16),
        pltpu.VMEM((order, cols), BF16),
        pltpu.VMEM((order, cols), BF16),
        pltpu.VMEM((order, cols), BF16),
    ]


def call(kernel, outs, scratch_shapes, operands, flops, identity=None):
    space = pl.BlockSpec(memory_space=pltpu.VMEM)
    more = {} if identity is None else dict(collective_id=identity, has_side_effects=True)
    return pl.pallas_call(
        kernel,
        out_shape=[jax.ShapeDtypeStruct(shape, F32) for shape in outs],
        in_specs=[space] * len(operands),
        out_specs=[space] * len(outs),
        scratch_shapes=scratch_shapes,
        compiler_params=pltpu.CompilerParams(vmem_limit_bytes=48 * 1024 * 1024, **more),
        cost_estimate=pl.CostEstimate(flops=flops, bytes_accessed=0, transcendentals=0),
    )(*operands)


def flags(*shape):
    return pltpu.SemaphoreType.DMA(shape)


def b_step(matrix, step):
    rows, cols = matrix.shape
    order = JOINED * PANEL
    column, other, mate = call(
        functools.partial(gather_kernel, step),
        [(4, rows, cols), (4, rows, cols), (rows, cols)],
        [flags(2, 2), flags(2), flags(2, 2), flags(2, 2), flags(2), flags(2), flags(5), flags(5)],
        [matrix], 10**10, 2 * step,
    )
    (half,) = call(
        functools.partial(center_kernel, step), [(rows, cols)], scratch(order, cols),
        [column, other, matrix, mate], 10**10,
    )
    (solved,) = call(
        functools.partial(share_kernel, step), [(2, rows, cols)],
        [flags(2, 2), flags(2), flags(2), flags(2)], [half], 10**10, 2 * step + 1,
    )
    (result,) = call(
        functools.partial(update_kernel, step), [(rows, cols)],
        [pltpu.VMEM((order, cols), BF16), pltpu.VMEM((order, cols), BF16)],
        [matrix, column, solved], 10**9,
    )
    return result


def a_steps(matrix, other):
    order = STEPS_A * PANEL
    cols = matrix.shape[1]
    row = jnp.concatenate([matrix[:order], other[:order]], 1)
    row = lax.all_gather(lax.all_gather(row, "z")[0], "core")[0]
    over = lax.all_gather(row[:, :cols], "y")
    mine = lax.dynamic_index_in_dim(over, lax.axis_index("z"), 0, keepdims=False)
    around = lax.all_gather(jnp.stack([mine, over[0]]), "x")
    column = lax.dynamic_slice_in_dim(around[:, 0], 2 * lax.axis_index("core"), 2, 0)
    return call(
        a_kernel, [matrix.shape, other.shape], scratch(order, cols),
        [matrix, other, column, row[:, :cols], row[:, cols:], around[0, 1]], 10**10,
    )


def squares(value):
    return jnp.sum(value * value)


def total_of(values):
    tile = (8, 128)
    corner = jnp.zeros(tile, F32).at[0, : len(values)].set(jnp.stack(values))
    (total,) = call(
        sum_kernel, [tile],
        [pltpu.VMEM((7, *tile), F32), pltpu.VMEM((15, *tile), F32), pltpu.VMEM(tile, F32), flags(7), flags(7), flags(15), flags(15)],
        [corner], 10**9, 2 * (STEPS_B // JOINED),
    )
    return [total[0, place] for place in range(len(values))]


def body(a_matrix, b_matrix, c_matrix):
    a_swept, c_swept = a_steps(a_matrix, c_matrix)
    b_inverse = b_matrix
    for step in range(STEPS_B // JOINED):
        b_inverse = b_step(b_inverse, step)
    b_squares, inv_squares = total_of([squares(b_matrix), squares(b_inverse)])
    scale = jnp.sqrt(jnp.sqrt(inv_squares / b_squares))
    b_next = 0.5 * (scale * b_matrix + b_inverse / scale)
    return (a_swept, c_swept, b_next)


def solution(mesh):
    finer = Mesh(mesh.devices.reshape(4, 2, 4, 4), AXES)
    placed = (P(ROW, COL), P(ROW, COL), P(ROW, COL))
    return jax.shard_map(body, mesh=finer, in_specs=placed, out_specs=placed, check_vma=False)
```

time: 2120 us -> 527 us (0.25)
  waiting for transfers between devices: 1740 us -> 134 us
  Pallas kernels: 0 us -> 352 us
  matrix products: 185 us -> 0 us
  local copies, waits for them, and re-layouts: 80.5 us -> 18.3 us
  other arithmetic: 42.6 us -> 6.34 us
  blocking collectives: 31.1 us -> 0 us
    all_gather x34 -> x4, waiting for transfers between devices: 1570 us -> 134 us  [the longest x2 85.3 us: a_steps(): row = lax.all_gather(lax.all_gather(row, 'z')[0], 'core')[0]]
    pallas_call x0 -> x18, Pallas kernels: none -> 352 us  [call(): pl.pallas_call(kernel, out_shape=[jax.ShapeDtypeStruct(shape, F32) for sh...]
    dot_general x254 -> x0, matrix products: 185 us -> none  [the longest x108 74.2 us: pivot_inverse(): jnp.dot(unit, approx, precision=EXACT, preferred_element_type=jnp.float32)]
    psum x2 -> x0, waiting for transfers between devices: 167 us -> none  [spread(): return lax.psum(kept, axis)]
    gather x18 -> x0, local copies, waits for them, and re-layouts: 42.2 us -> none  [pivot_inverse(): scaling = 1.0 / jnp.sqrt(jnp.diagonal(pivot))]
    psum x4 -> x0, blocking collectives: 31.1 us -> none  [over_axes(): return functools.reduce(lax.psum, axes, shard)]
  transfers between devices with their start and end apart: 36 -> 4, of which waited for: 36 -> 3; matrix products, arithmetic and copies ran while one was open for 4% -> 1% of each run, Pallas kernels for 0% -> 64%
where the time goes in v1:
time: 527 us
  Pallas kernels  352 us (67%)
  waiting for transfers between devices  134 us (25%)
  local copies, waits for them, and re-layouts  18.3 us (3%)
  between operations  15.3 us (3%)
  other arithmetic  6.34 us (1%)
    pallas_call x18, Pallas kernels, call(): pl.pallas_call(kernel, out_shape=[jax.ShapeDtypeStruct(shape, F32) for sh...  352 us
    all_gather x2, waiting for transfers between devices, a_steps(): row = lax.all_gather(lax.all_gather(row, 'z')[0], 'core')[0]  85.3 us
    all_gather x1, waiting for transfers between devices, a_steps(): over = lax.all_gather(row[:, :cols], 'y')  49.1 us
  transfers between devices with their start and end apart: 4, of which 3 were waited for; matrix products, arithmetic and copies ran while one was open for 1% of the time, Pallas kernels for 64%

profile of v1, /device:TPU:1, one launch (start us, length us, event | category | flops | bytes accessed | tf_op | source)
XLA Modules:
  0.0 526.9 jit_solution(12628780706080186318)
XLA Ops:
  7.2 1.0 slice-done.1
  8.6 1.2 pad_maximum_fusion.1
  9.9 69.3 %all-gather.9.cloned.1.call-done = f32[2048,768]{1,0:T(8,128)} async-done(((f32[512,768]{1,0:T(8,128)}), f32[2048,768]{1,0:T(8,128)}) %all-gather.9.cloned.1.call-update) | async-done | bytes 6291472 | tf_op jit(solution)/shard_map/all_gather | solution.py:460
  79.2 2.7 slice.66
  81.9 16.0 %all-gather.15.cloned.1.call-done = f32[1024,768]{1,0:T(8,128)} async-done(((f32[512,768]{1,0:T(8,128)}), f32[1024,768]{1,0:T(8,128)}) %all-gather.15.cloned.1.call-update) | async-done | bytes 3145744 | tf_op jit(solution)/shard_map/all_gather | solution.py:460
  97.9 2.3 slice.67.row
  100.2 49.1 %all-gather.11.cloned.1.call-done = f32[2048,512]{1,0:T(8,128)} async-done(((f32[512,512]{1,0:T(8,128)}), f32[2048,512]{1,0:T(8,128)}) %all-gather.11.cloned.1.call-update) | async-done | bytes 4194320 | tf_op jit(solution)/shard_map/all_gather | solution.py:461
  149.3 1.3 constant_dynamic-slice_fusion
  150.6 1.3 slice_bitcast_fusion.1
  151.9 1.5 pad_maximum_fusion
  153.4 1.0 copy-done
  154.4 30.8 %shard_map.59 = (f32[4,512,256]{2,1,0:T(8,128)S(1)}, f32[4,512,256]{2,1,0:T(8,128)S(1)}, f32[512,256]{1,0:T(8,128)S(1)}) custom-call(f32[512,256]{1,0:T(8,128)S(1)} %copy-done), custom_call_target="tpu_custom_call" | custom-call | flops 10000000000 | tf_op jit(solution)/shard_map/pallas_call | solution.py:416
  185.2 23.0 %shard_map.60.half = f32[512,256]{1,0:T(8,128)S(1)} custom-call(f32[4,512,256]{2,1,0:T(8,128)S(1)} %get-tuple-element.31.mine.column, f32[4,512,256]{2,1,0:T(8,128)S(1)} %get-tuple-element.32.other, f32[512,256]{1,0:T(8,128)S(1)} %copy-done, f32[512,256]{1,0:T(8,128)S(1)} %get-tuple-element.33.mate), custom_call_target="tpu_custom_call" | custom-call | flops 10000000000 | tf_op jit(solution)/shard_map/pallas_call | solution.py:416
  208.2 11.5 %shard_map.61.solved = f32[2,512,256]{2,1,0:T(8,128)S(1)} custom-call(f32[512,256]{1,0:T(8,128)S(1)} %shard_map.60.half), custom_call_target="tpu_custom_call" | custom-call | flops 10000000000 | tf_op jit(solution)/shard_map/pallas_call | solution.py:416
  219.7 1.3 shard_map.62.matrix
  221.1 49.8 %shard_map.63 = (f32[4,512,256]{2,1,0:T(8,128)S(1)}, f32[4,512,256]{2,1,0:T(8,128)S(1)}, f32[512,256]{1,0:T(8,128)S(1)}) custom-call(f32[512,256]{1,0:T(8,128)S(1)} %shard_map.62.matrix), custom_call_target="tpu_custom_call" | custom-call | flops 10000000000 | tf_op jit(solution)/shard_map/pallas_call | solution.py:416
  270.9 46.8 %shard_map.65.solved = f32[2,512,256]{2,1,0:T(8,128)S(1)} custom-call(f32[512,256]{1,0:T(8,128)S(1)} %shard_map.64.half), custom_call_target="tpu_custom_call" | custom-call | flops 10000000000 | tf_op jit(solution)/shard_map/pallas_call | solution.py:416
  317.7 1.3 shard_map.66.matrix
  319.0 36.2 %shard_map.67 = (f32[4,512,256]{2,1,0:T(8,128)S(1)}, f32[4,512,256]{2,1,0:T(8,128)S(1)}, f32[512,256]{1,0:T(8,128)S(1)}) custom-call(f32[512,256]{1,0:T(8,128)S(1)} %shard_map.66.matrix), custom_call_target="tpu_custom_call" | custom-call | flops 10000000000 | tf_op jit(solution)/shard_map/pallas_call | solution.py:416
  355.2 44.2 %shard_map.69.solved = f32[2,512,256]{2,1,0:T(8,128)S(1)} custom-call(f32[512,256]{1,0:T(8,128)S(1)} %shard_map.68.half), custom_call_target="tpu_custom_call" | custom-call | flops 10000000000 | tf_op jit(solution)/shard_map/pallas_call | solution.py:416
  399.4 1.4 shard_map.70.matrix
  400.7 29.1 %shard_map.71 = (f32[4,512,256]{2,1,0:T(8,128)S(1)}, f32[4,512,256]{2,1,0:T(8,128)S(1)}, f32[512,256]{1,0:T(8,128)S(1)}) custom-call(f32[512,256]{1,0:T(8,128)S(1)} %shard_map.70.matrix), custom_call_target="tpu_custom_call" | custom-call | flops 10000000000 | tf_op jit(solution)/shard_map/pallas_call | solution.py:416
  429.9 40.2 %shard_map.73.solved = f32[2,512,256]{2,1,0:T(8,128)S(1)} custom-call(f32[512,256]{1,0:T(8,128)S(1)} %shard_map.72.half), custom_call_target="tpu_custom_call" | custom-call | flops 10000000000 | tf_op jit(solution)/shard_map/pallas_call | solution.py:416
  470.1 1.4 shard_map.74
  472.9 1.3 maximum_bitcast_fusion
  474.2 18.5 %shard_map.75 = f32[8,128]{1,0:T(8,128)S(1)} custom-call(f32[8,128]{1,0:T(8,128)S(1)} %scatter.4.value), custom_call_target="tpu_custom_call" | custom-call | flops 1000000000 | tf_op jit(solution)/shard_map/pallas_call | solution.py:416
  495.5 1.1 slice.70.other_row
  496.6 1.3 slice_bitcast_fusion.pivot
  497.9 2.6 slice.69
  500.6 1.5 dynamic-slice_bitcast_fusion.column
  502.1 1.1 copy-done.2
  503.5 16.9 %shard_map.58 = (f32[1024,512]{1,0:T(8,128)}, f32[1024,256]{1,0:T(8,128)}) custom-call(f32[1024,512]{1,0:T(8,128)S(1)} %copy-done.2, f32[1024,256]{1,0:T(8,128)S(1)} %copy-done.3, f32[2,512,512]{2,1,0:T(8,128)} %dynamic-slice_bitcast_fusion.column, f32[512,512]{1,0:T(8,128)S(1)} %copy-done.1, f32[512,256]{1,0:T(8,128)S(1)} %slice.70.other_row, ...), custom_call_target="tpu_custom_call" | custom-call | flops 10000000000 | tf_op jit(solution)/shard_map/pallas_call | solution.py:416
  (26 shorter events, 3.9 us)
Async XLA Ops:
  7.2 1.0 slice-start.1
  7.2 1.4 slice-start
  7.2 72.0 %all-gather.9.cloned.1.call-start = ((), (), s32[]{:S(2)}) async-start(), calls=%async_computation | async-start | bytes 7864320 | tf_op jit(solution)/shard_map/all_gather | solution.py:460
  9.8 88.1 %all-gather.15.cloned.1.call-start = ((), (), s32[]{:S(2)}) async-start(), calls=%async_computation.3 | async-start | bytes 4718592 | tf_op jit(solution)/shard_map/all_gather | solution.py:460
  81.8 67.5 %all-gather.11.cloned.1.call-start = ((), (), s32[]{:S(2)}) async-start(), calls=%async_computation.1 | async-start | bytes 5242880 | tf_op jit(solution)/shard_map/all_gather | solution.py:461
  100.2 396.4 %all-gather.13.cloned.1.call-start = ((), (), s32[]{:S(2)}) async-start(), calls=%async_computation.2 | async-start | bytes 10485760 | tf_op jit(solution)/shard_map/all_gather | solution.py:463
  153.4 1.0 copy-start
  500.6 1.6 copy-start.1
  500.6 2.7 copy-start.2
  500.6 2.9 copy-start.3
Sparse Core Ops, SparseCore 0:
  10.2 68.8 all-gather.8
  82.0 15.8 all-gather.14
  100.3 48.9 all-gather.10
  153.5 89.8 all-gather.12

commit v2 on v1

v2 whole, which is shorter than its diff:
```python
import functools

import jax
import jax.numpy as jnp
from jax import lax
from jax.experimental import pallas as pl
from jax.experimental.pallas import tpu as pltpu
from jax.sharding import Mesh
from jax.sharding import PartitionSpec as P

PANEL = 256
SQUARINGS = 5
STEPS_A = 2
STEPS_B = 16
JOINED = 4
AXES = ("z", "core", "y", "x")
ROW = ("z", "core")
COL = ("y", "x")
F32 = jnp.float32
BF16 = jnp.bfloat16


def halves(value):
    high = value.astype(BF16)
    return high, (value - high.astype(F32)).astype(BF16)


def product(left, right):
    return jnp.dot(left, right, preferred_element_type=F32)


def triple(left, right_high, right_low):
    high, low = halves(left)
    return product(high, right_high) + product(high, right_low) + product(low, right_high)


def pivot_inverse(pivot):
    shape = (PANEL, PANEL)
    unit = lax.broadcasted_iota(jnp.int32, shape, 0) == lax.broadcasted_iota(jnp.int32, shape, 1)
    diagonal = jnp.where(unit, pivot, 0.0)
    down = 1.0 / jnp.sqrt(jnp.sum(diagonal, axis=1, keepdims=True))
    across = 1.0 / jnp.sqrt(jnp.sum(diagonal, axis=0, keepdims=True))
    scaled = pivot * down * across
    ceiling = jnp.max(jnp.sum(jnp.abs(scaled), axis=1, keepdims=True), axis=0, keepdims=True)
    eye = jnp.where(unit, 1.0, 0.0)
    power = eye - scaled / ceiling
    total = eye + power
    high, low = halves(power)
    power = product(high, high) + product(high, low) + product(low, high)
    for turn in range(SQUARINGS - 1):
        high, low = halves(jnp.concatenate([power, total], 0))
        both = product(high, high[:PANEL]) + product(high, low[:PANEL]) + product(low, high[:PANEL])
        power = both[:PANEL]
        total = total + both[PANEL:]
    high, low = halves(power)
    total = total + triple(total, high, low)
    return total / ceiling * down * across


def composite(count, table, fresh, fresh_high, fresh_low):
    @pl.loop(0, count)
    def _(p):
        here = pl.ds(pl.multiple_of(p * PANEL, PANEL), PANEL)
        inverse = pivot_inverse(table[here, here])
        high, low = halves(table[here, :])
        fresh[...] = triple(inverse, high, low)
        fresh[:, here] = inverse
        high, low = halves(fresh[...])
        fresh_high[...] = high
        fresh_low[...] = low

        @pl.loop(0, count)
        def _(q):
            @pl.when(q != p)
            def _():
                there = pl.ds(pl.multiple_of(q * PANEL, PANEL), PANEL)
                column = table[there, here]
                table[there, here] = jnp.zeros((PANEL, PANEL), F32)
                table[there, :] = table[there, :] - triple(column, fresh_high[...], fresh_low[...])

        table[here, :] = fresh[...]


def left_side(matrix, result, piece, row_base, col_base, order, solved_high, solved_low):
    rows, cols = matrix.shape

    @pl.loop(0, rows // PANEL)
    def _(r):
        start = pl.multiple_of(r * PANEL, PANEL)
        there = pl.ds(start, PANEL)
        down = row_base + start + lax.broadcasted_iota(jnp.int32, (PANEL, PANEL), 0)
        total = None
        for q in range(order // PANEL):
            unit = down == q * PANEL + lax.broadcasted_iota(jnp.int32, (PANEL, PANEL), 1)
            column = piece(start, q) - jnp.where(unit, 1.0, 0.0)
            among = pl.ds(q * PANEL, PANEL)
            part = triple(column, solved_high[among, :cols], solved_low[among, :cols])
            total = part if total is None else total + part
        base = matrix[there, :]
        if col_base is not None:
            inside = jnp.logical_and(col_base >= 0, col_base < order)
            across = col_base + lax.broadcasted_iota(jnp.int32, (PANEL, cols), 1)
            begin = row_base + start + lax.broadcasted_iota(jnp.int32, (PANEL, cols), 0)
            base = jnp.where(inside, jnp.where(begin == across, 1.0, 0.0), base)
        result[there, :] = base - total


def center_kernel(step, mine, other, matrix, mate, half, table, fresh, fresh_high, fresh_low, right_high, right_low):
    core = lax.axis_index("core")
    rows = matrix.shape[0]
    order = JOINED * PANEL
    base = (lax.axis_index("y") - step) * order + lax.axis_index("x") * matrix.shape[1]
    pair = (pl.ds(0, rows), pl.ds(rows, rows))

    @pl.when(lax.axis_index("z") == step)
    def _():
        for at in range(2):

            @pl.when(core == at)
            def _():
                for q in range(JOINED):
                    table[pair[at], q * PANEL : (q + 1) * PANEL] = mine[q]
                for q in range(2):
                    across = 2 * (1 - at) + q
                    table[pair[1 - at], across * PANEL : (across + 1) * PANEL] = other[q]
                    table[across * PANEL : (across + 1) * PANEL, pair[at]] = mine[across].T

        composite(JOINED, table, fresh, fresh_high, fresh_low)
        inside = jnp.logical_and(base >= 0, base < order)
        for first, source in ((core * rows, matrix), ((1 - core) * rows, mate)):
            shape = source.shape
            unit = first + lax.broadcasted_iota(jnp.int32, shape, 0) == base + lax.broadcasted_iota(jnp.int32, shape, 1)
            high, low = halves(jnp.where(inside, jnp.where(unit, 1.0, 0.0), source[...]))
            there = pl.ds(pl.multiple_of(first, rows), rows)
            right_high[there, :] = high
            right_low[there, :] = low
        for q in range(rows // PANEL):
            there = pl.ds(pl.multiple_of(core * rows + q * PANEL, PANEL), PANEL)
            half[q * PANEL : (q + 1) * PANEL, :] = triple(table[there, :], right_high[...], right_low[...])


def center_both_kernel(step, mine, other, matrix, mate, strips, a_top, c_top, half, a_solved, table, fresh, fresh_high, fresh_low, right_high, right_low, *a_scratch):
    center_kernel(step, mine, other, matrix, mate, half, table, fresh, fresh_high, fresh_low, right_high, right_low)
    a_table, a_fresh, a_fresh_high, a_fresh_low, a_right_high, a_right_low = a_scratch

    @pl.when(jnp.logical_and(lax.axis_index("z") == 0, lax.axis_index("core") == 0))
    def _():
        order, cols = a_top.shape
        a_table[...] = strips[0]
        composite(STEPS_A, a_table, a_fresh, a_fresh_high, a_fresh_low)
        base = (lax.axis_index("y") * 4 + lax.axis_index("x")) * cols
        unit = lax.broadcasted_iota(jnp.int32, (order, cols), 0) == base + lax.broadcasted_iota(jnp.int32, (order, cols), 1)
        high, low = halves(jnp.where(base < order, jnp.where(unit, 1.0, 0.0), a_top[...]))
        a_right_high[:, :cols] = high
        a_right_low[:, :cols] = low
        high, low = halves(c_top[...])
        a_right_high[:, cols:] = high
        a_right_low[:, cols:] = low
        for q in range(STEPS_A):
            there = slice(q * PANEL, (q + 1) * PANEL)
            a_solved[there, :] = triple(a_table[there, :], a_right_high[...], a_right_low[...])


def update_kernel(step, matrix, column, solved, result, solved_high, solved_low):
    order = JOINED * PANEL
    rows = matrix.shape[0]
    row_base = (lax.axis_index("z") - step) * order + lax.axis_index("core") * rows
    col_base = (lax.axis_index("y") - step) * order + lax.axis_index("x") * matrix.shape[1]
    for core in range(2):
        high, low = halves(solved[core])
        solved_high[core * rows : (core + 1) * rows, :] = high
        solved_low[core * rows : (core + 1) * rows, :] = low
    piece = lambda start, q: column[q, pl.ds(start, PANEL), :]
    left_side(matrix, result, piece, row_base, col_base, order, solved_high, solved_low)


def a_update_kernel(matrix, other, strips, solved, result, other_result, solved_high, solved_low):
    order = STEPS_A * PANEL
    cols = matrix.shape[1]
    row_base = (lax.axis_index("z") * 2 + lax.axis_index("core")) * matrix.shape[0]
    col_base = (lax.axis_index("y") * 4 + lax.axis_index("x")) * cols
    high, low = halves(solved[...])
    solved_high[...] = high
    solved_low[...] = low

    def piece(start, q):
        among = pl.ds(pl.multiple_of(lax.rem(start, order), PANEL), PANEL)
        return strips[start // order, pl.ds(q * PANEL, PANEL), among].T

    left_side(matrix, result, piece, row_base, col_base, order, solved_high.at[:, :cols], solved_low.at[:, :cols])
    left_side(other, other_result, piece, row_base, None, order, solved_high.at[:, cols:], solved_low.at[:, cols:])


CHUNKS = 4
AHEAD = (0, 1)
BEHIND = (2, 3)


def ring(index, by):
    return lax.rem(index + by, 4)


def send(source, target, sent, received, where):
    return pltpu.make_async_remote_copy(
        src_ref=source, dst_ref=target, send_sem=sent, recv_sem=received,
        device_id=where, device_id_type=pl.DeviceIdType.MESH,
    )


def greet(neighbours, tells=None, teller_of=None, told=None):
    barrier = pltpu.get_barrier_semaphore()
    for where in neighbours:
        pl.semaphore_signal(barrier, inc=1, device_id=where, device_id_type=pl.DeviceIdType.MESH)
    if tells is not None:

        @pl.when(tells)
        def _():
            pl.semaphore_signal(barrier, inc=1, device_id=teller_of, device_id_type=pl.DeviceIdType.MESH)

    if told is None:
        pl.semaphore_wait(barrier, len(neighbours))
    else:

        @pl.when(told)
        def _():
            pl.semaphore_wait(barrier, len(neighbours) + 1)

        @pl.when(jnp.logical_not(told))
        def _():
            pl.semaphore_wait(barrier, len(neighbours))


def chunk(h, rows=512):
    return pl.ds(h * (rows // CHUNKS), rows // CHUNKS)


def both(left, right):
    return left if right is True else jnp.logical_and(left, right)


def spread(axis, step, source, landing, sent, received, follow, active=True):
    place = lax.axis_index(axis)
    apart = lax.rem(place - step + 4, 4)
    up, down = {axis: ring(place, 1)}, {axis: ring(place, 3)}

    def copy(ref, h, side):
        return send(ref.at[chunk(h)], landing.at[chunk(h)], sent.at[side, h], received.at[h], (up, down)[side])

    def begin():
        @pl.when(both(apart == 0, active))
        def _():
            for one, two in zip(AHEAD + BEHIND, BEHIND + AHEAD):
                copy(source, one, 0).start()
                copy(source, two, 1).start()
            for h in range(CHUNKS):
                follow(h, source)

    def relay():
        def take(order, onward, side):
            for h in order:
                copy(landing, h, 0).wait_recv()
                if h in onward:
                    copy(landing, h, side).start()
                follow(h, landing)

        @pl.when(both(apart == 1, active))
        def _():
            take(AHEAD + BEHIND, AHEAD, 0)

        @pl.when(both(apart == 3, active))
        def _():
            take(BEHIND + AHEAD, BEHIND, 1)

        @pl.when(both(apart == 2, active))
        def _():
            take((0, 2, 1, 3), (), 0)

    def finish():
        @pl.when(both(apart == 0, active))
        def _():
            for h in range(CHUNKS):
                copy(source, h, 0).wait_send()
                copy(source, h, 1).wait_send()

        @pl.when(both(apart == 1, active))
        def _():
            for h in AHEAD:
                copy(landing, h, 0).wait_send()

        @pl.when(both(apart == 3, active))
        def _():
            for h in BEHIND:
                copy(landing, h, 1).wait_send()

    return apart, begin, relay, finish


def nothing(h, ref):
    pass


def gather(step, matrix, column, other, mate, y_sent, y_got, x_sent, x_got, far_sent, far_got, core_sent, core_got):
    x = lax.axis_index("x")
    core = lax.axis_index("core")
    right, left, far = ring(x, 1), ring(x, 3), ring(x, 2)
    partner = {"core": 1 - core}
    center = lax.axis_index("z") == step
    swap = send(matrix, mate, core_sent.at[2], core_got.at[2], partner)

    def sideways(h, ref):
        return [
            send(ref.at[chunk(h)], column.at[x, chunk(h)], x_sent.at[0, h], x_got.at[0, h], {"x": right}),
            send(ref.at[chunk(h)], column.at[x, chunk(h)], x_sent.at[1, h], x_got.at[1, h], {"x": left}),
        ]

    def follow(h, ref):
        for copy in sideways(h, ref):
            copy.start()

    apart, begin, relay, finish = spread("y", step, matrix, column.at[x], y_sent, y_got, follow)

    def start():
        begin()

        @pl.when(center)
        def _():
            swap.start()

    def give(place, ref):
        slot = lax.rem(place, 2)
        return send(ref, other.at[slot], core_sent.at[slot], core_got.at[slot], partner)

    def maybe_give(place, ref, also=True):
        @pl.when(both(jnp.logical_and(center, place // 2 == core), also))
        def _():
            give(place, ref).start()

    def arrive(place, h, received):
        ref = column.at[place, chunk(h)]
        send(ref, ref, x_sent.at[0, h], received, {"x": right}).wait_recv()

    def pass_on(h):
        place, where = (left, right) if h in AHEAD else (right, left)
        ref = column.at[place, chunk(h)]
        return send(ref, ref, far_sent.at[h], far_got.at[h], {"x": where})

    def middle():
        relay()
        maybe_give(x, matrix, apart == 0)
        maybe_give(x, column.at[x], apart != 0)

        @pl.when(apart == 0)
        def _():
            column[x] = matrix[...]

        for one, two in zip(AHEAD, BEHIND):
            arrive(left, one, x_got.at[0, one])
            pass_on(one).start()
            arrive(right, two, x_got.at[1, two])
            pass_on(two).start()
        for one, two in zip(AHEAD, BEHIND):
            arrive(right, one, x_got.at[1, one])
            arrive(left, two, x_got.at[0, two])
        maybe_give(left, column.at[left])
        maybe_give(right, column.at[right])
        for h in range(CHUNKS):
            arrive(far, h, far_got.at[h])
        maybe_give(far, column.at[far])

    def end():
        finish()
        for h in range(CHUNKS):
            for copy in sideways(h, matrix):
                copy.wait_send()
            pass_on(h).wait_send()

        @pl.when(center)
        def _():
            swap.wait()
            give(0, matrix).wait()
            give(1, matrix).wait()

    return start, middle, end


def gather_neighbours():
    x, y = lax.axis_index("x"), lax.axis_index("y")
    return [{"y": ring(y, 1)}, {"y": ring(y, 3)}, {"x": ring(x, 1)}, {"x": ring(x, 3)}, {"core": 1 - lax.axis_index("core")}]


def gather_kernel(step, matrix, column, other, mate, *flags_of):
    greet(gather_neighbours())
    for act in gather(step, matrix, column, other, mate, *flags_of):
        act()


def gather_first_kernel(step, matrix, a_top, column, other, mate, seed, *flags_of):
    *flags_of, seed_sent, seed_got = flags_of
    z, core, y, x = (lax.axis_index(axis) for axis in AXES)
    home = jnp.logical_and(z == 0, core == 0)
    goal = jnp.logical_and(z == y, core == x // 2)
    stays = jnp.logical_and(home, goal)
    goes = jnp.logical_and(home, jnp.logical_not(goal))
    comes = jnp.logical_and(goal, jnp.logical_not(home))
    greet(gather_neighbours(), comes, {"z": 0, "core": 0}, goes)
    copy = send(a_top, seed, seed_sent, seed_got, {"z": y, "core": x // 2})

    @pl.when(goes)
    def _():
        copy.start()

    for act in gather(step, matrix, column, other, mate, *flags_of):
        act()

    @pl.when(stays)
    def _():
        seed[...] = a_top[...]

    @pl.when(goes)
    def _():
        copy.wait_send()

    @pl.when(comes)
    def _():
        copy.wait_recv()


def gather_last_kernel(step, matrix, a_solved, column, other, mate, a_shared, *flags_of):
    *flags_of, z_sent, z_got, pass_sent, pass_got = flags_of
    z, core = lax.axis_index("z"), lax.axis_index("core")
    partner = {"core": 1 - core}
    greet(gather_neighbours() + [{"z": ring(z, 1)}, {"z": ring(z, 3)}])

    def give(h, ref):
        return send(ref.at[chunk(h)], a_shared.at[chunk(h)], pass_sent.at[h], pass_got.at[h], partner)

    def follow(h, ref):
        give(h, ref).start()

    apart, begin, relay, finish = spread("z", 0, a_solved, a_shared, z_sent, z_got, follow, core == 0)
    start, middle, end = gather(step, matrix, column, other, mate, *flags_of)
    start()
    begin()
    middle()
    relay()

    @pl.when(jnp.logical_and(apart == 0, core == 0))
    def _():
        a_shared[...] = a_solved[...]

    end()
    finish()

    @pl.when(core == 0)
    def _():
        for h in range(CHUNKS):
            give(h, a_solved).wait_send()

    @pl.when(core == 1)
    def _():
        for h in range(CHUNKS):
            give(h, a_solved).wait_recv()


def share(step, half, solved, z_sent, z_got, core_sent, core_got):
    core = lax.axis_index("core")
    partner = {"core": 1 - core}

    def give(h, ref):
        return send(ref.at[chunk(h)], solved.at[core, chunk(h)], core_sent.at[h], core_got.at[h], partner)

    def follow(h, ref):
        give(h, ref).start()

    apart, begin, relay, finish = spread("z", step, half, solved.at[core], z_sent, z_got, follow)

    def end():
        @pl.when(apart == 0)
        def _():
            solved[core] = half[...]

        finish()
        for h in range(CHUNKS):
            give(h, half).wait_send()
            ref = solved.at[1 - core, chunk(h)]
            send(ref, ref, core_sent.at[h], core_got.at[h], partner).wait_recv()

    return begin, relay, end


def share_neighbours():
    z = lax.axis_index("z")
    return [{"z": ring(z, 1)}, {"z": ring(z, 3)}, {"core": 1 - lax.axis_index("core")}]


def share_kernel(step, half, solved, *flags_of):
    greet(share_neighbours())
    for act in share(step, half, solved, *flags_of):
        act()


def share_first_kernel(step, half, seed, solved, strip, *flags_of):
    *flags_of, y_sent, y_got = flags_of
    y = lax.axis_index("y")
    holds = lax.axis_index("core") == lax.axis_index("x") // 2
    greet(share_neighbours() + [{"y": ring(y, 1)}, {"y": ring(y, 3)}])
    begin, relay, end = share(step, half, solved, *flags_of)
    apart, also_begin, also_relay, also_finish = spread("y", lax.axis_index("z"), seed, strip, y_sent, y_got, nothing, holds)
    begin()
    also_begin()
    relay()
    also_relay()

    @pl.when(jnp.logical_and(holds, apart == 0))
    def _():
        strip[...] = seed[...]

    end()
    also_finish()


def share_second_kernel(step, half, strip, solved, strips, *flags_of):
    *flags_of, x_sent, x_got = flags_of
    x, core = lax.axis_index("x"), lax.axis_index("core")
    greet(share_neighbours() + [{"x": ring(x, 1)}, {"x": ring(x, 3)}])
    begin, relay, end = share(step, half, solved, *flags_of)
    pair = [spread("x", 2 * core + s, strip, strips.at[s], x_sent.at[s], x_got.at[s], nothing) for s in range(2)]
    begin()
    for one in pair:
        one[1]()
    relay()
    for one in pair:
        one[2]()
    for s in range(2):

        @pl.when(pair[s][0] == 0)
        def _():
            strips[s] = strip[...]

    end()
    for one in pair:
        one[3]()


def sum_kernel(value, total, first, second, between, first_sent, first_got, second_sent, second_got):
    z, core, y, x = (lax.axis_index(axis) for axis in AXES)
    line, plane = z * 2 + core, y * 4 + x

    def of_line(by):
        place = lax.rem(line + by, 8)
        return {"z": place // 2, "core": lax.rem(place, 2)}

    def of_plane(by):
        place = lax.rem(plane + by, 16)
        return {"y": place // 4, "x": lax.rem(place, 4)}

    greet([of_line(by) for by in range(1, 8)] + [of_plane(by) for by in range(1, 16)])
    copies = [send(value, first.at[by - 1], first_sent.at[by - 1], first_got.at[by - 1], of_line(by)) for by in range(1, 8)]
    for copy in copies:
        copy.start()
    for copy in copies:
        copy.wait()
    result = value[...]
    for by in range(7):
        result = result + first[by]
    between[...] = result
    copies = [send(between, second.at[by - 1], second_sent.at[by - 1], second_got.at[by - 1], of_plane(by)) for by in range(1, 16)]
    for copy in copies:
        copy.start()
    for copy in copies:
        copy.wait()
    for by in range(15):
        result = result + second[by]
    total[...] = result


def scratch(order, cols):
    return [
        pltpu.VMEM((order, order), F32),
        pltpu.VMEM((PANEL, order), F32),
        pltpu.VMEM((PANEL, order), BF16),
        pltpu.VMEM((PANEL, order), BF16),
        *pair_of(order, cols),
    ]


def pair_of(order, cols):
    return [pltpu.VMEM((order, cols), BF16), pltpu.VMEM((order, cols), BF16)]


def call(kernel, outs, scratch_shapes, operands, flops, identity=None):
    space = pl.BlockSpec(memory_space=pltpu.VMEM)
    more = {} if identity is None else dict(collective_id=identity, has_side_effects=True)
    return pl.pallas_call(
        kernel,
        out_shape=[jax.ShapeDtypeStruct(shape, F32) for shape in outs],
        in_specs=[space] * len(operands),
        out_specs=[space] * len(outs),
        scratch_shapes=scratch_shapes,
        compiler_params=pltpu.CompilerParams(vmem_limit_bytes=48 * 1024 * 1024, **more),
        cost_estimate=pl.CostEstimate(flops=flops, bytes_accessed=0, transcendentals=0),
    )(*operands)


def flags(*shape):
    return pltpu.SemaphoreType.DMA(shape)


def sweeps(a_matrix, b_matrix, c_matrix):
    rows, cols = b_matrix.shape
    order = JOINED * PANEL
    a_order = STEPS_A * PANEL
    a_cols, c_cols = a_matrix.shape[1], c_matrix.shape[1]
    a_top, c_top = a_matrix[:a_order], c_matrix[:a_order]
    side = (a_order, a_cols)
    panel = [(4, rows, cols), (2, rows, cols), (rows, cols)]
    panel_flags = [flags(2, CHUNKS), flags(CHUNKS), flags(2, CHUNKS), flags(2, CHUNKS), flags(CHUNKS), flags(CHUNKS), flags(3), flags(3)]
    shared = [(2, rows, cols)]
    shared_flags = [flags(2, CHUNKS), flags(CHUNKS), flags(CHUNKS), flags(CHUNKS)]
    more_flags = [flags(2, CHUNKS), flags(CHUNKS)]
    matrix = b_matrix
    for step in range(STEPS_B // JOINED):
        last = STEPS_B // JOINED - 1
        bound = lambda kernel: functools.partial(kernel, step)
        if step == 0:
            column, other, mate, seed = call(
                bound(gather_first_kernel), panel + [side], panel_flags + [pltpu.SemaphoreType.DMA, pltpu.SemaphoreType.DMA],
                [matrix, a_top], 10**10, 2 * step,
            )
        elif step == last:
            column, other, mate, a_shared = call(
                bound(gather_last_kernel), panel + [(a_order, a_cols + c_cols)],
                panel_flags + more_flags + [flags(CHUNKS), flags(CHUNKS)], [matrix, a_solved], 10**10, 2 * step,
            )
        else:
            column, other, mate = call(bound(gather_kernel), panel, panel_flags, [matrix], 10**10, 2 * step)
        operands = [column, other, matrix, mate]
        if step == last - 1:
            half, a_solved = call(
                bound(center_both_kernel), [(rows, cols), (a_order, a_cols + c_cols)],
                scratch(order, cols) + scratch(a_order, a_cols + c_cols), operands + [strips, a_top, c_top], 10**10,
            )
        else:
            (half,) = call(bound(center_kernel), [(rows, cols)], scratch(order, cols), operands, 10**10)
        if step == 0:
            solved, strip = call(bound(share_first_kernel), shared + [side], shared_flags + more_flags, [half, seed], 10**10, 2 * step + 1)
        elif step == 1:
            solved, strips = call(
                bound(share_second_kernel), shared + [(2, *side)],
                shared_flags + [flags(2, 2, CHUNKS), flags(2, CHUNKS)], [half, strip], 10**10, 2 * step + 1,
            )
        else:
            (solved,) = call(bound(share_kernel), shared, shared_flags, [half], 10**10, 2 * step + 1)
        (matrix,) = call(bound(update_kernel), [(rows, cols)], pair_of(order, cols), [matrix, column, solved], 10**9)
    a_swept, c_swept = call(
        a_update_kernel, [a_matrix.shape, c_matrix.shape], pair_of(a_order, a_cols + c_cols),
        [a_matrix, c_matrix, strips, a_shared], 10**10,
    )
    return a_swept, c_swept, matrix


def squares(value):
    return jnp.sum(value * value)


def total_of(values):
    tile = (8, 128)
    corner = jnp.zeros(tile, F32).at[0, : len(values)].set(jnp.stack(values))
    (total,) = call(
        sum_kernel, [tile],
        [pltpu.VMEM((7, *tile), F32), pltpu.VMEM((15, *tile), F32), pltpu.VMEM(tile, F32), flags(7), flags(7), flags(15), flags(15)],
        [corner], 10**9, 2 * (STEPS_B // JOINED),
    )
    return [total[0, place] for place in range(len(values))]


def body(a_matrix, b_matrix, c_matrix):
    a_swept, c_swept, b_inverse = sweeps(a_matrix, b_matrix, c_matrix)
    b_squares, inv_squares = total_of([squares(b_matrix), squares(b_inverse)])
    scale = jnp.sqrt(jnp.sqrt(inv_squares / b_squares))
    b_next = 0.5 * (scale * b_matrix + b_inverse / scale)
    return (a_swept, c_swept, b_next)


def solution(mesh):
    finer = Mesh(mesh.devices.reshape(4, 2, 4, 4), AXES)
    placed = (P(ROW, COL), P(ROW, COL), P(ROW, COL))
    return jax.shard_map(body, mesh=finer, in_specs=placed, out_specs=placed, check_vma=False)
```

time: 527 us -> 347 us (0.66)
  waiting for transfers between devices: 134 us -> 0 us
  Pallas kernels: 352 us -> 332 us
  between operations: 15.3 us -> 2.27 us
  local copies, waits for them, and re-layouts: 18.3 us -> 7.81 us
    all_gather x4 -> x0, waiting for transfers between devices: 134 us -> none  [the longest x2 85.3 us: a_steps(): row = lax.all_gather(lax.all_gather(row, 'z')[0], 'core')[0]]
    pallas_call x18, Pallas kernels: 352 us -> 332 us  [call(): pl.pallas_call(kernel, out_shape=[jax.ShapeDtypeStruct(shape, F32) for sh...]
    slice x9 -> x2, local copies, waits for them, and re-layouts: 11.2 us -> 1.39 us  [sweeps(): a_top, c_top = (a_matrix[:a_order], c_matrix[:a_order])]
  transfers between devices with their start and end apart: 4 -> 0, of which waited for: 3 -> 0; matrix products, arithmetic and copies ran while one was open for 1% -> 0% of each run, Pallas kernels for 64% -> 0%
where the time goes in v2:
time: 347 us; the launch traced here: 346 us
  Pallas kernels  332 us (96%)
  local copies, waits for them, and re-layouts  7.81 us (2%)
  other arithmetic  3.7 us (1%)
    pallas_call x18, Pallas kernels, call(): pl.pallas_call(kernel, out_shape=[jax.ShapeDtypeStruct(shape, F32) for sh...  332 us

profile of v2, /device:TPU:1, one launch (start us, length us, event | category | flops | bytes accessed | tf_op | source)
XLA Modules:
  0.0 346.2 jit_solution(5291937363890671349)
XLA Ops:
  0.6 1.4 slice.28.a_top
  2.0 0.0 copy-done
  2.0 26.4 %shard_map.58 = (f32[4,512,256]{2,1,0:T(8,128)}, f32[2,512,256]{2,1,0:T(8,128)S(1)}, f32[512,256]{1,0:T(8,128)S(1)}, f32[512,512]{1,0:T(8,128)S(1)}) custom-call(f32[512,256]{1,0:T(8,128)S(1)} %copy-done, f32[512,512]{1,0:T(8,128)S(1)} %slice.28.a_top), custom_call_target="tpu_custom_call" | custom-call | flops 10000000000 | tf_op jit(solution)/shard_map/pallas_call | solution.py:594
  28.4 1.6 copy-done.3
  30.0 23.2 %shard_map.59.half = f32[512,256]{1,0:T(8,128)S(1)} custom-call(f32[4,512,256]{2,1,0:T(8,128)S(1)} %copy-done.3, f32[2,512,256]{2,1,0:T(8,128)S(1)} %get-tuple-element.38.other, f32[512,256]{1,0:T(8,128)S(1)} %copy-done, f32[512,256]{1,0:T(8,128)S(1)} %get-tuple-element.39.mate), custom_call_target="tpu_custom_call" | custom-call | flops 10000000000 | tf_op jit(solution)/shard_map/pallas_call | solution.py:594
  53.1 18.1 %shard_map.60 = (f32[2,512,256]{2,1,0:T(8,128)S(1)}, f32[512,512]{1,0:T(8,128)S(1)}) custom-call(f32[512,256]{1,0:T(8,128)S(1)} %shard_map.59.half, f32[512,512]{1,0:T(8,128)S(1)} %get-tuple-element.40.seed), custom_call_target="tpu_custom_call" | custom-call | flops 10000000000 | tf_op jit(solution)/shard_map/pallas_call | solution.py:594
  71.2 0.0 copy-done.4
  71.2 1.3 shard_map.61.matrix
  72.6 28.5 %shard_map.62 = (f32[4,512,256]{2,1,0:T(8,128)S(1)}, f32[2,512,256]{2,1,0:T(8,128)S(1)}, f32[512,256]{1,0:T(8,128)S(1)}) custom-call(f32[512,256]{1,0:T(8,128)S(1)} %shard_map.61.matrix), custom_call_target="tpu_custom_call" | custom-call | flops 10000000000 | tf_op jit(solution)/shard_map/pallas_call | solution.py:594
  101.1 57.5 %shard_map.64 = (f32[2,512,256]{2,1,0:T(8,128)S(1)}, f32[2,512,512]{2,1,0:T(8,128)S(1)}) custom-call(f32[512,256]{1,0:T(8,128)S(1)} %shard_map.63.half, f32[512,512]{1,0:T(8,128)S(1)} %get-tuple-element.45.strip), custom_call_target="tpu_custom_call" | custom-call | flops 10000000000 | tf_op jit(solution)/shard_map/pallas_call | solution.py:594
  158.6 1.3 copy-done.9
  160.0 1.3 shard_map.65.matrix
  161.3 0.0 copy-start.8
  161.3 32.5 %shard_map.66 = (f32[4,512,256]{2,1,0:T(8,128)S(1)}, f32[2,512,256]{2,1,0:T(8,128)S(1)}, f32[512,256]{1,0:T(8,128)S(1)}) custom-call(f32[512,256]{1,0:T(8,128)S(1)} %shard_map.65.matrix), custom_call_target="tpu_custom_call" | custom-call | flops 10000000000 | tf_op jit(solution)/shard_map/pallas_call | solution.py:594
  193.9 0.0 copy-start.1
  193.9 1.3 copy-done.1
  195.2 0.0 copy-done.8
  195.2 2.2 shard_map.67
  197.5 39.3 %shard_map.68.solved = f32[2,512,256]{2,1,0:T(8,128)S(1)} custom-call(f32[512,256]{1,0:T(8,128)S(1)} %get-tuple-element.51.half), custom_call_target="tpu_custom_call" | custom-call | flops 10000000000 | tf_op jit(solution)/shard_map/pallas_call | solution.py:594
  236.8 0.0 copy-done.2
  236.8 1.4 shard_map.69.matrix
  238.2 27.9 %shard_map.70 = (f32[4,512,256]{2,1,0:T(8,128)}, f32[2,512,256]{2,1,0:T(8,128)S(1)}, f32[512,256]{1,0:T(8,128)S(1)}, f32[512,768]{1,0:T(8,128)S(1)}) custom-call(f32[512,256]{1,0:T(8,128)S(1)} %shard_map.69.matrix, f32[512,768]{1,0:T(8,128)S(1)} %get-tuple-element.52.a_solved), custom_call_target="tpu_custom_call" | custom-call | flops 10000000000 | tf_op jit(solution)/shard_map/pallas_call | solution.py:594
  266.1 1.6 copy-done.5
  267.7 49.7 %shard_map.73.solved = f32[2,512,256]{2,1,0:T(8,128)S(1)} custom-call(f32[512,256]{1,0:T(8,128)S(1)} %shard_map.72.half), custom_call_target="tpu_custom_call" | custom-call | flops 10000000000 | tf_op jit(solution)/shard_map/pallas_call | solution.py:594
  317.4 1.3 shard_map.74
  318.8 0.7 multiply_reduce_fusion
  319.5 0.7 multiply_reduce_fusion.1
  320.2 1.4 maximum_bitcast_fusion
  321.6 14.2 %shard_map.75 = f32[8,128]{1,0:T(8,128)S(1)} custom-call(f32[8,128]{1,0:T(8,128)S(1)} %scatter.4.value), custom_call_target="tpu_custom_call" | custom-call | flops 1000000000 | tf_op jit(solution)/shard_map/pallas_call | solution.py:594
  335.8 0.6 fusion
  337.8 0.9 add_multiply_fusion
  338.7 7.6 %shard_map.71 = (f32[1024,512]{1,0:T(8,128)}, f32[1024,256]{1,0:T(8,128)}) custom-call(f32[1024,512]{1,0:T(8,128)S(1)} %copy-done.7, f32[1024,256]{1,0:T(8,128)S(1)} %copy-done.8, f32[2,512,512]{2,1,0:T(8,128)} %copy-done.9, f32[512,768]{1,0:T(8,128)S(1)} %get-tuple-element.53.solved), custom_call_target="tpu_custom_call" | custom-call | flops 10000000000 | tf_op jit(solution)/shard_map/pallas_call | solution.py:594
  (14 shorter events, 0.1 us)
Async XLA Ops:
  0.6 1.4 copy-start
  28.4 1.6 copy-start.3
  53.1 18.1 %copy-start.4 = (f32[4,512,256]{2,1,0:T(8,128)S(1)}, f32[4,512,256]{2,1,0:T(8,128)}, u32[]{:S(2)}) copy-start(f32[4,512,256]{2,1,0:T(8,128)} %get-tuple-element.37.mine.column) | copy-start | bytes 6291460
  158.6 1.3 copy-start.9
  161.3 33.9 %copy-start.8 = (f32[1024,256]{1,0:T(8,128)S(1)}, f32[1024,256]{1,0:T(8,128)}, u32[]{:S(2)}) copy-start(f32[1024,256]{1,0:T(8,128)} %other.1) | copy-start | bytes 3145732
  193.9 1.3 copy-start.1
  197.5 39.3 %copy-start.2 = (f32[4,512,256]{2,1,0:T(8,128)S(1)}, f32[4,512,256]{2,1,0:T(8,128)}, u32[]{:S(2)}) copy-start(f32[4,512,256]{2,1,0:T(8,128)} %copy-done.1) | copy-start | bytes 6291460
  266.1 1.6 copy-start.5
  267.7 49.7 %copy-start.6 = (f32[4,512,256]{2,1,0:T(8,128)S(1)}, f32[4,512,256]{2,1,0:T(8,128)}, u32[]{:S(2)}) copy-start(f32[4,512,256]{2,1,0:T(8,128)} %get-tuple-element.56.mine.column) | copy-start | bytes 6291460
  321.6 17.0 %copy-start.7 = (f32[1024,512]{1,0:T(8,128)S(1)}, f32[1024,512]{1,0:T(8,128)}, u32[]{:S(2)}) copy-start(f32[1024,512]{1,0:T(8,128)} %matrix.7) | copy-start | bytes 6291460

commit v3 on v2

v3 whole, which is shorter than its diff:
```python
import functools

import jax
import jax.numpy as jnp
from jax import lax
from jax.experimental import pallas as pl
from jax.experimental.pallas import tpu as pltpu
from jax.sharding import Mesh
from jax.sharding import PartitionSpec as P

PANEL = 256
SQUARINGS = 5
STEPS_A = 2
STEPS_B = 16
JOINED = 4
AXES = ("z", "core", "y", "x")
ROW = ("z", "core")
COL = ("y", "x")
F32 = jnp.float32
BF16 = jnp.bfloat16


def halves(value):
    high = value.astype(BF16)
    return high, (value - high.astype(F32)).astype(BF16)


def product(left, right):
    return jnp.dot(left, right, preferred_element_type=F32)


def triple(left, right_high, right_low):
    high, low = halves(left)
    return product(high, right_high) + product(high, right_low) + product(low, right_high)


def pivot_inverse(pivot):
    shape = (PANEL, PANEL)
    unit = lax.broadcasted_iota(jnp.int32, shape, 0) == lax.broadcasted_iota(jnp.int32, shape, 1)
    diagonal = jnp.where(unit, pivot, 0.0)
    down = 1.0 / jnp.sqrt(jnp.sum(diagonal, axis=1, keepdims=True))
    across = 1.0 / jnp.sqrt(jnp.sum(diagonal, axis=0, keepdims=True))
    scaled = pivot * down * across
    ceiling = jnp.max(jnp.sum(jnp.abs(scaled), axis=1, keepdims=True), axis=0, keepdims=True)
    eye = jnp.where(unit, 1.0, 0.0)
    power = eye - scaled / ceiling
    total = eye + power
    high, low = halves(power)
    power = product(high, high) + product(high, low) + product(low, high)
    for turn in range(SQUARINGS - 1):
        high, low = halves(jnp.concatenate([power, total], 0))
        both = product(high, high[:PANEL]) + product(high, low[:PANEL]) + product(low, high[:PANEL])
        power = both[:PANEL]
        total = total + both[PANEL:]
    high, low = halves(power)
    total = total + triple(total, high, low)
    return total / ceiling * down * across


def composite(count, table, fresh, fresh_high, fresh_low):
    @pl.loop(0, count)
    def _(p):
        here = pl.ds(pl.multiple_of(p * PANEL, PANEL), PANEL)
        inverse = pivot_inverse(table[here, here])
        high, low = halves(table[here, :])
        fresh[...] = triple(inverse, high, low)
        fresh[:, here] = inverse
        high, low = halves(fresh[...])
        fresh_high[...] = high
        fresh_low[...] = low

        @pl.loop(0, count)
        def _(q):
            @pl.when(q != p)
            def _():
                there = pl.ds(pl.multiple_of(q * PANEL, PANEL), PANEL)
                column = table[there, here]
                table[there, here] = jnp.zeros((PANEL, PANEL), F32)
                table[there, :] = table[there, :] - triple(column, fresh_high[...], fresh_low[...])

        table[here, :] = fresh[...]


def left_side(matrix, result, piece, row_base, col_base, order, solved_high, solved_low):
    rows, cols = matrix.shape

    @pl.loop(0, rows // PANEL)
    def _(r):
        start = pl.multiple_of(r * PANEL, PANEL)
        there = pl.ds(start, PANEL)
        down = row_base + start + lax.broadcasted_iota(jnp.int32, (PANEL, PANEL), 0)
        total = None
        for q in range(order // PANEL):
            unit = down == q * PANEL + lax.broadcasted_iota(jnp.int32, (PANEL, PANEL), 1)
            column = piece(start, q) - jnp.where(unit, 1.0, 0.0)
            among = pl.ds(q * PANEL, PANEL)
            part = triple(column, solved_high[among, :cols], solved_low[among, :cols])
            total = part if total is None else total + part
        base = matrix[there, :]
        if col_base is not None:
            inside = jnp.logical_and(col_base >= 0, col_base < order)
            across = col_base + lax.broadcasted_iota(jnp.int32, (PANEL, cols), 1)
            begin = row_base + start + lax.broadcasted_iota(jnp.int32, (PANEL, cols), 0)
            base = jnp.where(inside, jnp.where(begin == across, 1.0, 0.0), base)
        result[there, :] = base - total


def center(step, mine, other, matrix, mate, half, table, fresh, fresh_high, fresh_low, right_high, right_low):
    core = lax.axis_index("core")
    rows = matrix.shape[0]
    order = JOINED * PANEL
    base = (lax.axis_index("y") - step) * order + lax.axis_index("x") * matrix.shape[1]
    pair = (pl.ds(0, rows), pl.ds(rows, rows))
    for at in range(2):

        @pl.when(core == at)
        def _():
            for q in range(JOINED):
                table[pair[at], q * PANEL : (q + 1) * PANEL] = mine[q]
            for q in range(2):
                across = 2 * (1 - at) + q
                table[pair[1 - at], across * PANEL : (across + 1) * PANEL] = other[q]
                table[across * PANEL : (across + 1) * PANEL, pair[at]] = mine[across].T

    composite(JOINED, table, fresh, fresh_high, fresh_low)
    inside = jnp.logical_and(base >= 0, base < order)
    for first, source in ((core * rows, matrix), ((1 - core) * rows, mate)):
        shape = source.shape
        unit = first + lax.broadcasted_iota(jnp.int32, shape, 0) == base + lax.broadcasted_iota(jnp.int32, shape, 1)
        high, low = halves(jnp.where(inside, jnp.where(unit, 1.0, 0.0), source[...]))
        there = pl.ds(pl.multiple_of(first, rows), rows)
        right_high[there, :] = high
        right_low[there, :] = low
    for q in range(rows // PANEL):
        there = pl.ds(pl.multiple_of(core * rows + q * PANEL, PANEL), PANEL)
        half[q * PANEL : (q + 1) * PANEL, :] = triple(table[there, :], right_high[...], right_low[...])


def a_center(strips, a_top, c_top, solved, table, fresh, fresh_high, fresh_low, right_high, right_low):
    order, cols = a_top.shape
    table[...] = strips[0]
    composite(STEPS_A, table, fresh, fresh_high, fresh_low)
    base = (lax.axis_index("y") * 4 + lax.axis_index("x")) * cols
    unit = lax.broadcasted_iota(jnp.int32, (order, cols), 0) == base + lax.broadcasted_iota(jnp.int32, (order, cols), 1)
    high, low = halves(jnp.where(base < order, jnp.where(unit, 1.0, 0.0), a_top[...]))
    right_high[:, :cols] = high
    right_low[:, :cols] = low
    high, low = halves(c_top[...])
    right_high[:, cols:] = high
    right_low[:, cols:] = low
    for q in range(STEPS_A):
        there = slice(q * PANEL, (q + 1) * PANEL)
        solved[there, :] = triple(table[there, :], right_high[...], right_low[...])


def update(step, matrix, column, solved, result, solved_high, solved_low):
    order = JOINED * PANEL
    rows = matrix.shape[0]
    row_base = (lax.axis_index("z") - step) * order + lax.axis_index("core") * rows
    col_base = (lax.axis_index("y") - step) * order + lax.axis_index("x") * matrix.shape[1]
    for core in range(2):
        high, low = halves(solved[core])
        solved_high[core * rows : (core + 1) * rows, :] = high
        solved_low[core * rows : (core + 1) * rows, :] = low
    piece = lambda start, q: column[q, pl.ds(start, PANEL), :]
    left_side(matrix, result, piece, row_base, col_base, order, solved_high, solved_low)


def a_update(matrix, other, strips, solved, solved_high, solved_low):
    order = STEPS_A * PANEL
    cols = matrix.shape[1]
    row_base = (lax.axis_index("z") * 2 + lax.axis_index("core")) * matrix.shape[0]
    col_base = (lax.axis_index("y") * 4 + lax.axis_index("x")) * cols
    high, low = halves(solved[...])
    solved_high[...] = high
    solved_low[...] = low

    def piece(start, q):
        among = pl.ds(pl.multiple_of(lax.rem(start, order), PANEL), PANEL)
        return strips[start // order, pl.ds(q * PANEL, PANEL), among].T

    left_side(matrix, matrix, piece, row_base, col_base, order, solved_high.at[:, :cols], solved_low.at[:, :cols])
    left_side(other, other, piece, row_base, None, order, solved_high.at[:, cols:], solved_low.at[:, cols:])


CHUNKS = 4
AHEAD = (0, 1)
BEHIND = (2, 3)


def ring(index, by):
    return lax.rem(index + by, 4)


def send(source, target, sent, received, where):
    return pltpu.make_async_remote_copy(
        src_ref=source, dst_ref=target, send_sem=sent, recv_sem=received,
        device_id=where, device_id_type=pl.DeviceIdType.MESH,
    )


def greet(neighbours):
    barrier = pltpu.get_barrier_semaphore()
    for where in neighbours:
        pl.semaphore_signal(barrier, inc=1, device_id=where, device_id_type=pl.DeviceIdType.MESH)
    pl.semaphore_wait(barrier, len(neighbours))


def chunk(h, rows=512):
    return pl.ds(h * (rows // CHUNKS), rows // CHUNKS)


def both(left, right):
    return left if right is True else jnp.logical_and(left, right)


def spread(axis, step, source, landing, sent, received, follow, active=True):
    place = lax.axis_index(axis)
    apart = lax.rem(place - step + 4, 4)
    up, down = {axis: ring(place, 1)}, {axis: ring(place, 3)}

    def copy(ref, h, side):
        return send(ref.at[chunk(h)], landing.at[chunk(h)], sent.at[side, h], received.at[h], (up, down)[side])

    def begin():
        @pl.when(both(apart == 0, active))
        def _():
            for one, two in zip(AHEAD + BEHIND, BEHIND + AHEAD):
                copy(source, one, 0).start()
                copy(source, two, 1).start()
            for h in range(CHUNKS):
                follow(h, source)

    def relay():
        def take(order, onward, side):
            for h in order:
                copy(landing, h, 0).wait_recv()
                if h in onward:
                    copy(landing, h, side).start()
                follow(h, landing)

        @pl.when(both(apart == 1, active))
        def _():
            take(AHEAD + BEHIND, AHEAD, 0)

        @pl.when(both(apart == 3, active))
        def _():
            take(BEHIND + AHEAD, BEHIND, 1)

        @pl.when(both(apart == 2, active))
        def _():
            take((0, 2, 1, 3), (), 0)

    def finish():
        @pl.when(both(apart == 0, active))
        def _():
            for h in range(CHUNKS):
                copy(source, h, 0).wait_send()
                copy(source, h, 1).wait_send()

        @pl.when(both(apart == 1, active))
        def _():
            for h in AHEAD:
                copy(landing, h, 0).wait_send()

        @pl.when(both(apart == 3, active))
        def _():
            for h in BEHIND:
                copy(landing, h, 1).wait_send()

    return apart, begin, relay, finish


def nothing(h, ref):
    pass


def gather(step, matrix, column, other, mate, y_sent, y_got, x_sent, x_got, far_sent, far_got, core_sent, core_got):
    x = lax.axis_index("x")
    core = lax.axis_index("core")
    right, left, far = ring(x, 1), ring(x, 3), ring(x, 2)
    partner = {"core": 1 - core}
    centered = lax.axis_index("z") == step
    swap = send(matrix, mate, core_sent.at[2], core_got.at[2], partner)

    def sideways(h, ref):
        return [
            send(ref.at[chunk(h)], column.at[x, chunk(h)], x_sent.at[0, h], x_got.at[0, h], {"x": right}),
            send(ref.at[chunk(h)], column.at[x, chunk(h)], x_sent.at[1, h], x_got.at[1, h], {"x": left}),
        ]

    def follow(h, ref):
        for copy in sideways(h, ref):
            copy.start()

    apart, begin, relay, finish = spread("y", step, matrix, column.at[x], y_sent, y_got, follow)

    def start():
        begin()

        @pl.when(centered)
        def _():
            swap.start()

    def give(place, ref):
        slot = lax.rem(place, 2)
        return send(ref, other.at[slot], core_sent.at[slot], core_got.at[slot], partner)

    def maybe_give(place, ref, also=True):
        @pl.when(both(jnp.logical_and(centered, place // 2 == core), also))
        def _():
            give(place, ref).start()

    def arrive(place, h, received):
        ref = column.at[place, chunk(h)]
        send(ref, ref, x_sent.at[0, h], received, {"x": right}).wait_recv()

    def pass_on(h):
        place, where = (left, right) if h in AHEAD else (right, left)
        ref = column.at[place, chunk(h)]
        return send(ref, ref, far_sent.at[h], far_got.at[h], {"x": where})

    def middle():
        relay()
        maybe_give(x, matrix, apart == 0)
        maybe_give(x, column.at[x], apart != 0)

        @pl.when(apart == 0)
        def _():
            column[x] = matrix[...]

        for one, two in zip(AHEAD, BEHIND):
            arrive(left, one, x_got.at[0, one])
            pass_on(one).start()
            arrive(right, two, x_got.at[1, two])
            pass_on(two).start()
        for one, two in zip(AHEAD, BEHIND):
            arrive(right, one, x_got.at[1, one])
            arrive(left, two, x_got.at[0, two])
        maybe_give(left, column.at[left])
        maybe_give(right, column.at[right])
        for h in range(CHUNKS):
            arrive(far, h, far_got.at[h])
        maybe_give(far, column.at[far])

    def end():
        finish()
        for h in range(CHUNKS):
            for copy in sideways(h, matrix):
                copy.wait_send()
            pass_on(h).wait_send()

        @pl.when(centered)
        def _():
            swap.wait()
            give(0, matrix).wait()
            give(1, matrix).wait()

    return start, middle, end


def share(step, half, solved, z_sent, z_got, core_sent, core_got):
    core = lax.axis_index("core")
    partner = {"core": 1 - core}

    def give(h, ref):
        return send(ref.at[chunk(h)], solved.at[core, chunk(h)], core_sent.at[h], core_got.at[h], partner)

    def follow(h, ref):
        give(h, ref).start()

    apart, begin, relay, finish = spread("z", step, half, solved.at[core], z_sent, z_got, follow)

    def end():
        @pl.when(apart == 0)
        def _():
            solved[core] = half[...]

        finish()
        for h in range(CHUNKS):
            give(h, half).wait_send()
            ref = solved.at[1 - core, chunk(h)]
            send(ref, ref, core_sent.at[h], core_got.at[h], partner).wait_recv()

    return begin, relay, end


def peers():
    z, core, y, x = (lax.axis_index(axis) for axis in AXES)
    line, plane = z * 2 + core, y * 4 + x
    along, among = [], []
    for by in range(1, 8):
        place = lax.rem(line + by, 8)
        along.append({"z": place // 2, "core": lax.rem(place, 2)})
    for by in range(1, 16):
        place = lax.rem(plane + by, 16)
        among.append({"y": place // 4, "x": lax.rem(place, 4)})
    return along, among


def exchange(value, slots, sent, received, partners):
    copies = [send(value, slots.at[at], sent.at[at], received.at[at], where) for at, where in enumerate(partners)]
    for copy in copies:
        copy.start()
    for copy in copies:
        copy.wait()
    result = value[...]
    for at in range(len(partners)):
        result = result + slots[at]
    return result


def squares(value):
    return jnp.sum(jnp.sum(value * value, axis=0, keepdims=True), axis=1, keepdims=True)


def whole_kernel(a_hbm, b, c_hbm, a_out, c_out, b_out, *spaces):
    s = dict(zip(SPACES, spaces))
    z, core, y, x = (lax.axis_index(axis) for axis in AXES)
    a, c = s["a"], s["c"]
    a_order = STEPS_A * PANEL
    a_top, c_top = a.at[:a_order], c.at[:a_order]
    loads = [pltpu.make_async_copy(a_hbm, a, s["load"].at[0]), pltpu.make_async_copy(c_hbm, c, s["load"].at[1])]
    stores = [pltpu.make_async_copy(a, a_out, s["load"].at[0]), pltpu.make_async_copy(c, c_out, s["load"].at[1])]
    for copy in loads:
        copy.start()
    along, among = peers()
    greet(along + among)

    home = jnp.logical_and(z == 0, core == 0)
    holds = core == x // 2
    goal = jnp.logical_and(z == y, holds)
    stays = jnp.logical_and(home, goal)
    goes = jnp.logical_and(home, jnp.logical_not(goal))
    comes = jnp.logical_and(goal, jnp.logical_not(home))
    seeding = send(a_top, s["seed"], s["seed_sent"], s["seed_got"], {"z": y, "core": x // 2})
    partner = {"core": 1 - core}

    def a_give(h, ref):
        return send(ref.at[chunk(h)], s["a_shared"].at[chunk(h)], s["a_pass_sent"].at[h], s["a_pass_got"].at[h], partner)

    def a_follow(h, ref):
        a_give(h, ref).start()

    def along_y(source, active):
        return spread("y", z, source, s["strip"], s["ay_sent"], s["ay_got"], nothing, active)

    def along_x(active):
        return [
            spread("x", 2 * core + at, s["strip"], s["strips"].at[at], s["ax_sent"].at[at], s["ax_got"].at[at], nothing, active)
            for at in range(2)
        ]

    a_share = spread("z", 0, s["a_solved"], s["a_shared"], s["az_sent"], s["az_got"], a_follow, core == 0)

    def finish_a():
        a_update(a, c, s["strips"], s["a_shared"], s["a_solved_high"], s["a_solved_low"])
        for copy in stores:
            copy.start()

    matrix = b
    for step in range(STEPS_B // JOINED):
        column, other, mate, half, solved = (s[name].at[step] for name in ("column", "other", "mate", "half", "solved"))
        here, away = z == step, z != step
        start, middle, end = gather(step, matrix, column, other, mate, *(s[name].at[step] for name in GATHER_FLAGS))
        start()
        if step == 0:
            for copy in loads:
                copy.wait()

            @pl.when(goes)
            def _():
                seeding.start()

        middle()
        if step == 3:
            a_share[2]()
        end()
        if step == 0:

            @pl.when(goes)
            def _():
                seeding.wait_send()

            @pl.when(comes)
            def _():
                seeding.wait_recv()

            along_y(s["seed"], jnp.logical_and(holds, jnp.logical_not(stays)))[1]()
            along_y(a_top, stays)[1]()
        if step == 1:
            for one in along_x(True):
                one[1]()

        @pl.when(here)
        def _():
            center(step, column, other, matrix, mate, half, *(s[name] for name in ("table", "fresh", "fresh_high", "fresh_low", "right_high", "right_low")))

        if step == 0:
            along_y(s["seed"], jnp.logical_and(holds, away))[2]()
        if step == 1:
            for one in along_x(away):
                one[2]()
        if step == 2:

            @pl.when(home)
            def _():
                a_center(s["strips"], a_top, c_top, s["a_solved"], *(s[name] for name in ("a_table", "a_fresh", "a_fresh_high", "a_fresh_low", "a_right_high", "a_right_low")))

        if step == 3:
            @pl.when(jnp.logical_and(home, a_share[0] == 0))
            def _():
                s["a_shared"][...] = s["a_solved"][...]

            @pl.when(core == 1)
            def _():
                for h in range(CHUNKS):
                    a_give(h, s["a_solved"]).wait_recv()

            pl.when(away)(finish_a)

        begin, relay, close = share(step, half, solved, *(s[name].at[step] for name in SHARE_FLAGS))
        begin()
        relay()
        if step == 0:
            along_y(s["seed"], jnp.logical_and(holds, here))[2]()
            across = along_y(s["seed"], holds)

            @pl.when(stays)
            def _():
                s["strip"][...] = a_top[...]

            @pl.when(comes)
            def _():
                s["strip"][...] = s["seed"][...]

        if step == 1:
            for one in along_x(here):
                one[2]()
            for at, one in enumerate(along_x(True)):

                @pl.when(one[0] == 0)
                def _():
                    s["strips"][at] = s["strip"][...]

        if step == 3:
            pl.when(here)(finish_a)
        close()
        if step == 0:
            across[3]()
        if step == 1:
            for one in along_x(True):
                one[3]()
        update(step, matrix, column, solved, s["matrix"].at[step], s["solved_high"], s["solved_low"])
        matrix = s["matrix"].at[step]
        if step == 2:
            a_share[1]()

    lane = lax.broadcasted_iota(jnp.int32, (8, 128), 1)
    s["partial"][0] = jnp.where(lane == 0, squares(b[...]), squares(matrix[...]))
    s["partial"][1] = exchange(s["partial"].at[0], s["line"], s["line_sent"], s["line_got"], along)
    total = exchange(s["partial"].at[1], s["plane"], s["plane_sent"], s["plane_got"], among)
    scale = jnp.sqrt(jnp.sqrt(total[0:1, 1:2] / total[0:1, 0:1]))
    b_out[...] = 0.5 * (scale * b[...] + matrix[...] / scale)
    a_share[3]()

    @pl.when(core == 0)
    def _():
        for h in range(CHUNKS):
            a_give(h, s["a_solved"]).wait_send()

    for copy in stores:
        copy.wait()


GATHER_FLAGS = ("y_sent", "y_got", "x_sent", "x_got", "far_sent", "far_got", "core_sent", "core_got")
SHARE_FLAGS = ("z_sent", "z_got", "pass_sent", "pass_got")


def flags(*shape):
    return pltpu.SemaphoreType.DMA(shape)


def spaces_of(a_shape, b_shape, c_shape):
    steps = STEPS_B // JOINED
    order, a_order = JOINED * PANEL, STEPS_A * PANEL
    rows, cols = b_shape
    wide = a_shape[1] + c_shape[1]
    top = (a_order, a_shape[1])
    full = lambda *shape: pltpu.VMEM(shape, F32)
    short = lambda *shape: pltpu.VMEM(shape, BF16)
    ringed = (2, CHUNKS)
    return dict(
        a=full(*a_shape), c=full(*c_shape), load=flags(2),
        column=full(steps, 4, rows, cols), other=full(steps, 2, rows, cols), mate=full(steps, rows, cols),
        half=full(steps, rows, cols), solved=full(steps, 2, rows, cols), matrix=full(steps, rows, cols),
        table=full(order, order), fresh=full(PANEL, order), fresh_high=short(PANEL, order), fresh_low=short(PANEL, order),
        right_high=short(order, cols), right_low=short(order, cols), solved_high=short(order, cols), solved_low=short(order, cols),
        seed=full(*top), strip=full(*top), strips=full(2, *top), a_solved=full(a_order, wide), a_shared=full(a_order, wide),
        a_table=full(a_order, a_order), a_fresh=full(PANEL, a_order), a_fresh_high=short(PANEL, a_order), a_fresh_low=short(PANEL, a_order),
        a_right_high=short(a_order, wide), a_right_low=short(a_order, wide), a_solved_high=short(a_order, wide), a_solved_low=short(a_order, wide),
        partial=full(2, 8, 128), line=full(7, 8, 128), plane=full(15, 8, 128),
        y_sent=flags(steps, *ringed), y_got=flags(steps, CHUNKS), x_sent=flags(steps, *ringed), x_got=flags(steps, *ringed),
        far_sent=flags(steps, CHUNKS), far_got=flags(steps, CHUNKS), core_sent=flags(steps, 3), core_got=flags(steps, 3),
        z_sent=flags(steps, *ringed), z_got=flags(steps, CHUNKS), pass_sent=flags(steps, CHUNKS), pass_got=flags(steps, CHUNKS),
        seed_sent=pltpu.SemaphoreType.DMA, seed_got=pltpu.SemaphoreType.DMA,
        ay_sent=flags(*ringed), ay_got=flags(CHUNKS), ax_sent=flags(2, *ringed), ax_got=flags(2, CHUNKS),
        az_sent=flags(*ringed), az_got=flags(CHUNKS), a_pass_sent=flags(CHUNKS), a_pass_got=flags(CHUNKS),
        line_sent=flags(7), line_got=flags(7), plane_sent=flags(15), plane_got=flags(15),
    )


SPACES = tuple(spaces_of((1, 1), (1, 1), (1, 1)))


def body(a_matrix, b_matrix, c_matrix):
    held = pl.BlockSpec(memory_space=pltpu.VMEM)
    left = pl.BlockSpec(memory_space=pl.ANY)
    shapes = (a_matrix.shape, b_matrix.shape, c_matrix.shape)
    a_swept, c_swept, b_next = pl.pallas_call(
        whole_kernel,
        out_shape=[jax.ShapeDtypeStruct(shapes[at], F32) for at in (0, 2, 1)],
        in_specs=[left, held, left],
        out_specs=[left, left, held],
        scratch_shapes=list(spaces_of(*shapes).values()),
        compiler_params=pltpu.CompilerParams(vmem_limit_bytes=63 * 1024 * 1024, collective_id=0, has_side_effects=True),
    )(a_matrix, b_matrix, c_matrix)
    return (a_swept, c_swept, b_next)


def solution(mesh):
    finer = Mesh(mesh.devices.reshape(4, 2, 4, 4), AXES)
    placed = (P(ROW, COL), P(ROW, COL), P(ROW, COL))
    return jax.shard_map(body, mesh=finer, in_specs=placed, out_specs=placed, check_vma=False)
```

time: 347 us -> 287 us (0.83)
  Pallas kernels: 332 us -> 281 us
  other arithmetic: 3.7 us -> 0 us
    pallas_call x18 -> x1, Pallas kernels: 332 us -> 281 us  [body(): pl.pallas_call(whole_kernel, out_shape=[jax.ShapeDtypeStruct(shapes[at],...]
where the time goes in v3:
time: 287 us
  Pallas kernels  281 us (98%)
  local copies, waits for them, and re-layouts  4.97 us (2%)
    pallas_call x1, Pallas kernels, body(): pl.pallas_call(whole_kernel, out_shape=[jax.ShapeDtypeStruct(shapes[at],...  281 us

profile of v3, /device:TPU:1, one launch (start us, length us, event | category | flops | bytes accessed | tf_op | source)
XLA Modules:
  0.0 286.5 jit_solution(16998428911317826204)
XLA Ops:
  0.6 280.9 %shard_map.58 = (f32[1024,512]{1,0:T(8,128)}, f32[1024,256]{1,0:T(8,128)}, f32[512,256]{1,0:T(8,128)}) custom-call(f32[1024,512]{1,0:T(8,128)} %a_hbm.1, f32[512,256]{1,0:T(8,128)} %b.1, f32[1024,256]{1,0:T(8,128)} %c_hbm.1), custom_call_target="tpu_custom_call" | custom-call | tf_op jit(solution)/shard_map/pallas_call | solution.py:620
  281.5 0.0 copy-start
  281.6 0.0 copy-start.1
  281.6 3.2 %copy.9 = f32[1024,512]{1,0:T(8,128)} copy(f32[1024,512]{1,0:T(8,128)} %get-tuple-element.6) | data formatting | bytes 4194304
  284.8 0.0 copy-done
  284.8 1.0 copy.10
  285.7 0.0 copy-done.1
  285.7 0.8 copy.11
Async XLA Ops:
  281.5 3.2 %copy-start = (f32[1024,256]{1,0:T(8,128)S(1)}, f32[1024,256]{1,0:T(8,128)}, u32[]{:S(2)}) copy-start(f32[1024,256]{1,0:T(8,128)} %get-tuple-element.7) | copy-start | bytes 3145732
  281.6 4.2 %copy-start.1 = (f32[512,256]{1,0:T(8,128)S(1)}, f32[512,256]{1,0:T(8,128)}, u32[]{:S(2)}) copy-start(f32[512,256]{1,0:T(8,128)} %get-tuple-element.8) | copy-start | bytes 1572868

commit v4 on v3

--- a/solution.py
+++ b/solution.py
@@ -29,9 +29,18 @@
     return jnp.dot(left, right, preferred_element_type=F32)
 
 
+def summed(high, low, right_high, right_low):
+    return product(high, right_high) + product(high, right_low) + product(low, right_high)
+
+
 def triple(left, right_high, right_low):
-    high, low = halves(left)
-    return product(high, right_high) + product(high, right_low) + product(low, right_high)
+    return summed(*halves(left), right_high, right_low)
+
+
+def by_rows(high, low, right_high, right_low):
+    cut = high.shape[0] // 2
+    parts = [summed(high[at], low[at], right_high, right_low) for at in (slice(None, cut), slice(cut, None))]
+    return jnp.concatenate(parts, 0)
 
 
 def pivot_inverse(pivot):
@@ -46,38 +55,37 @@
     power = eye - scaled / ceiling
     total = eye + power
     high, low = halves(power)
-    power = product(high, high) + product(high, low) + product(low, high)
+    power = by_rows(high, low, high, low)
     for turn in range(SQUARINGS - 1):
-        high, low = halves(jnp.concatenate([power, total], 0))
-        both = product(high, high[:PANEL]) + product(high, low[:PANEL]) + product(low, high[:PANEL])
-        power = both[:PANEL]
-        total = total + both[PANEL:]
-    high, low = halves(power)
-    total = total + triple(total, high, low)
+        high, low = halves(power)
+        total_high, total_low = halves(total)
+        pair = summed(high, low, jnp.concatenate([high, total_high], 1), jnp.concatenate([low, total_low], 1))
+        power = pair[:, :PANEL]
+        total = total + pair[:, PANEL:]
+    total = total + by_rows(*halves(total), *halves(power))
     return total / ceiling * down * across
 
 
 def composite(count, table, fresh, fresh_high, fresh_low):
+    width = table.shape[1] // 2
+
     @pl.loop(0, count)
     def _(p):
         here = pl.ds(pl.multiple_of(p * PANEL, PANEL), PANEL)
         inverse = pivot_inverse(table[here, here])
-        high, low = halves(table[here, :])
-        fresh[...] = triple(inverse, high, low)
+        fresh[...] = triple(inverse, *halves(table[here, :]))
         fresh[:, here] = inverse
         high, low = halves(fresh[...])
         fresh_high[...] = high
         fresh_low[...] = low
-
-        @pl.loop(0, count)
-        def _(q):
-            @pl.when(q != p)
-            def _():
-                there = pl.ds(pl.multiple_of(q * PANEL, PANEL), PANEL)
-                column = table[there, here]
-                table[there, here] = jnp.zeros((PANEL, PANEL), F32)
-                table[there, :] = table[there, :] - triple(column, fresh_high[...], fresh_low[...])
-
+        others = [pl.ds(pl.multiple_of(lax.rem(p + by, count) * PANEL, PANEL), PANEL) for by in range(1, count)]
+        high, low = halves(jnp.concatenate([table[there, here] for there in others], 0))
+        for there in others:
+            table[there, here] = jnp.zeros((PANEL, PANEL), F32)
+        for cols in (slice(0, width), slice(width, 2 * width)):
+            taken = summed(high, low, fresh_high[:, cols], fresh_low[:, cols])
+            for at, there in enumerate(others):
+                table[there, cols] = table[there, cols] - taken[at * PANEL : (at + 1) * PANEL]
         table[here, :] = fresh[...]
 
 
@@ -183,9 +191,9 @@
     left_side(other, other, piece, row_base, None, order, solved_high.at[:, cols:], solved_low.at[:, cols:])
 
 
-CHUNKS = 4
-AHEAD = (0, 1)
-BEHIND = (2, 3)
+CHUNKS = 8
+AHEAD = tuple(range(CHUNKS // 2))
+BEHIND = tuple(range(CHUNKS // 2, CHUNKS))
 
 
 def ring(index, by):
@@ -249,7 +257,7 @@
 
         @pl.when(both(apart == 2, active))
         def _():
-            take((0, 2, 1, 3), (), 0)
+            take([h for two in zip(AHEAD, BEHIND) for h in two], (), 0)
 
     def finish():
         @pl.when(both(apart == 0, active))

time: 287 us -> 266 us (0.927)
  Pallas kernels: 281 us -> 261 us
    pallas_call x1, Pallas kernels: 281 us -> 261 us  [body(): pl.pallas_call(whole_kernel, out_shape=[jax.ShapeDtypeStruct(shapes[at],...]
where the time goes in v4:
time: 266 us
  Pallas kernels  261 us (98%)
  local copies, waits for them, and re-layouts  4.97 us (2%)
    pallas_call x1, Pallas kernels, body(): pl.pallas_call(whole_kernel, out_shape=[jax.ShapeDtypeStruct(shapes[at],...  261 us

profile of v4, /device:TPU:1, one launch (start us, length us, event | category | flops | bytes accessed | tf_op | source)
XLA Modules:
  0.0 266.1 jit_solution(3719062661468867781)
XLA Ops:
  0.6 260.5 %shard_map.58 = (f32[1024,512]{1,0:T(8,128)}, f32[1024,256]{1,0:T(8,128)}, f32[512,256]{1,0:T(8,128)}) custom-call(f32[1024,512]{1,0:T(8,128)} %a_hbm.1, f32[512,256]{1,0:T(8,128)} %b.1, f32[1024,256]{1,0:T(8,128)} %c_hbm.1), custom_call_target="tpu_custom_call" | custom-call | tf_op jit(solution)/shard_map/pallas_call | solution.py:628
  261.2 0.0 copy-start
  261.2 0.0 copy-start.1
  261.2 3.2 %copy.9 = f32[1024,512]{1,0:T(8,128)} copy(f32[1024,512]{1,0:T(8,128)} %get-tuple-element.6) | data formatting | bytes 4194304
  264.4 0.0 copy-done
  264.4 1.0 copy.10
  265.3 0.0 copy-done.1
  265.3 0.8 copy.11
Async XLA Ops:
  261.2 3.2 %copy-start = (f32[1024,256]{1,0:T(8,128)S(1)}, f32[1024,256]{1,0:T(8,128)}, u32[]{:S(2)}) copy-start(f32[1024,256]{1,0:T(8,128)} %get-tuple-element.7) | copy-start | bytes 3145732
  261.2 4.2 %copy-start.1 = (f32[512,256]{1,0:T(8,128)S(1)}, f32[512,256]{1,0:T(8,128)}, u32[]{:S(2)}) copy-start(f32[512,256]{1,0:T(8,128)} %get-tuple-element.8) | copy-start | bytes 1572868

commit v5 on v4

--- a/solution.py
+++ b/solution.py
@@ -43,7 +43,13 @@
     return jnp.concatenate(parts, 0)
 
 
-def pivot_inverse(pivot):
+def pivot_inverse(pivot, between=()):
+    parts = iter(between)
+
+    def fill():
+        for part in next(parts, ()):
+            part()
+
     shape = (PANEL, PANEL)
     unit = lax.broadcasted_iota(jnp.int32, shape, 0) == lax.broadcasted_iota(jnp.int32, shape, 1)
     diagonal = jnp.where(unit, pivot, 0.0)
@@ -53,40 +59,61 @@
     ceiling = jnp.max(jnp.sum(jnp.abs(scaled), axis=1, keepdims=True), axis=0, keepdims=True)
     eye = jnp.where(unit, 1.0, 0.0)
     power = eye - scaled / ceiling
+    fill()
     total = eye + power
     high, low = halves(power)
     power = by_rows(high, low, high, low)
+    fill()
     for turn in range(SQUARINGS - 1):
         high, low = halves(power)
         total_high, total_low = halves(total)
         pair = summed(high, low, jnp.concatenate([high, total_high], 1), jnp.concatenate([low, total_low], 1))
+        fill()
         power = pair[:, :PANEL]
         total = total + pair[:, PANEL:]
     total = total + by_rows(*halves(total), *halves(power))
     return total / ceiling * down * across
 
 
-def composite(count, table, fresh, fresh_high, fresh_low):
-    width = table.shape[1] // 2
-
-    @pl.loop(0, count)
+def composite(count, table, fresh, fresh_high, fresh_low, inverse_of):
+    inverse_of[...] = pivot_inverse(table[:PANEL, :PANEL])
+
+    def panel(p, more):
+        here = pl.ds(pl.multiple_of(p * PANEL, PANEL), PANEL)
+        others = [pl.ds(pl.multiple_of(lax.rem(p + by, count) * PANEL, PANEL), PANEL) for by in range(1, count)]
+        inverse = inverse_of[...]
+        inverse_high, inverse_low = halves(inverse)
+        high, low = halves(jnp.concatenate([table[there, here] for there in others], 0))
+
+        def row():
+            fresh[...] = summed(inverse_high, inverse_low, *halves(table[here, :]))
+            fresh[:, here] = inverse
+            fresh_high[...], fresh_low[...] = halves(fresh[...])
+            for there in others:
+                table[there, here] = jnp.zeros((PANEL, PANEL), F32)
+
+        def rest(at):
+            cols = slice(at * PANEL, (at + 1) * PANEL)
+            taken = summed(high, low, fresh_high[:, cols], fresh_low[:, cols])
+            for nth, there in enumerate(others):
+                table[there, cols] = table[there, cols] - taken[nth * PANEL : (nth + 1) * PANEL]
+
+        parts = [row] + [functools.partial(rest, at) for at in range(count)]
+        if more:
+            after = others[0]
+            solved = by_rows(inverse_high, inverse_low, *halves(table[here, after]))
+            block = table[after, after] - by_rows(high[:PANEL], low[:PANEL], *halves(solved))
+            inverse_of[...] = pivot_inverse(block, [(part,) for part in parts])
+        else:
+            for part in parts:
+                part()
+        table[here, :] = fresh[...]
+
+    @pl.loop(0, count - 1)
     def _(p):
-        here = pl.ds(pl.multiple_of(p * PANEL, PANEL), PANEL)
-        inverse = pivot_inverse(table[here, here])
-        fresh[...] = triple(inverse, *halves(table[here, :]))
-        fresh[:, here] = inverse
-        high, low = halves(fresh[...])
-        fresh_high[...] = high
-        fresh_low[...] = low
-        others = [pl.ds(pl.multiple_of(lax.rem(p + by, count) * PANEL, PANEL), PANEL) for by in range(1, count)]
-        high, low = halves(jnp.concatenate([table[there, here] for there in others], 0))
-        for there in others:
-            table[there, here] = jnp.zeros((PANEL, PANEL), F32)
-        for cols in (slice(0, width), slice(width, 2 * width)):
-            taken = summed(high, low, fresh_high[:, cols], fresh_low[:, cols])
-            for at, there in enumerate(others):
-                table[there, cols] = table[there, cols] - taken[at * PANEL : (at + 1) * PANEL]
-        table[here, :] = fresh[...]
+        panel(p, True)
+
+    panel(count - 1, False)
 
 
 def left_side(matrix, result, piece, row_base, col_base, order, solved_high, solved_low):
@@ -113,7 +140,7 @@
         result[there, :] = base - total
 
 
-def center(step, mine, other, matrix, mate, half, table, fresh, fresh_high, fresh_low, right_high, right_low):
+def center(step, mine, other, matrix, mate, half, table, fresh, fresh_high, fresh_low, inverse_of, right_high, right_low):
     core = lax.axis_index("core")
     rows = matrix.shape[0]
     order = JOINED * PANEL
@@ -130,7 +157,7 @@
                 table[pair[1 - at], across * PANEL : (across + 1) * PANEL] = other[q]
                 table[across * PANEL : (across + 1) * PANEL, pair[at]] = mine[across].T
 
-    composite(JOINED, table, fresh, fresh_high, fresh_low)
+    composite(JOINED, table, fresh, fresh_high, fresh_low, inverse_of)
     inside = jnp.logical_and(base >= 0, base < order)
     for first, source in ((core * rows, matrix), ((1 - core) * rows, mate)):
         shape = source.shape
@@ -144,10 +171,10 @@
         half[q * PANEL : (q + 1) * PANEL, :] = triple(table[there, :], right_high[...], right_low[...])
 
 
-def a_center(strips, a_top, c_top, solved, table, fresh, fresh_high, fresh_low, right_high, right_low):
+def a_center(strips, a_top, c_top, solved, table, fresh, fresh_high, fresh_low, inverse_of, right_high, right_low):
     order, cols = a_top.shape
     table[...] = strips[0]
-    composite(STEPS_A, table, fresh, fresh_high, fresh_low)
+    composite(STEPS_A, table, fresh, fresh_high, fresh_low, inverse_of)
     base = (lax.axis_index("y") * 4 + lax.axis_index("x")) * cols
     unit = lax.broadcasted_iota(jnp.int32, (order, cols), 0) == base + lax.broadcasted_iota(jnp.int32, (order, cols), 1)
     high, low = halves(jnp.where(base < order, jnp.where(unit, 1.0, 0.0), a_top[...]))
@@ -422,18 +449,19 @@
     return jnp.sum(jnp.sum(value * value, axis=0, keepdims=True), axis=1, keepdims=True)
 
 
-def whole_kernel(a_hbm, b, c_hbm, a_out, c_out, b_out, *spaces):
+def whole_kernel(a_hbm, b_hbm, c_hbm, a_out, c_out, b_out, *spaces):
     s = dict(zip(SPACES, spaces))
     z, core, y, x = (lax.axis_index(axis) for axis in AXES)
-    a, c = s["a"], s["c"]
+    a, b, c = s["a"], s["matrix"].at[0], s["c"]
     a_order = STEPS_A * PANEL
     a_top, c_top = a.at[:a_order], c.at[:a_order]
-    loads = [pltpu.make_async_copy(a_hbm, a, s["load"].at[0]), pltpu.make_async_copy(c_hbm, c, s["load"].at[1])]
-    stores = [pltpu.make_async_copy(a, a_out, s["load"].at[0]), pltpu.make_async_copy(c, c_out, s["load"].at[1])]
+    loads = [pltpu.make_async_copy(held, to, s["load"].at[at]) for at, (held, to) in enumerate([(b_hbm, b), (a_hbm, a), (c_hbm, c)])]
+    stores = [pltpu.make_async_copy(a, a_out, s["load"].at[1]), pltpu.make_async_copy(c, c_out, s["load"].at[2])]
     for copy in loads:
         copy.start()
     along, among = peers()
     greet(along + among)
+    loads[0].wait()
 
     home = jnp.logical_and(z == 0, core == 0)
     holds = core == x // 2
@@ -466,57 +494,64 @@
         for copy in stores:
             copy.start()
 
-    matrix = b
-    for step in range(STEPS_B // JOINED):
+    def both_of(*conditions):
+        return functools.reduce(jnp.logical_and, conditions)
+
+    @pl.loop(0, STEPS_B // JOINED)
+    def _(step):
+        first, second, third, last = (step == at for at in range(4))
+        matrix = s["matrix"].at[step]
         column, other, mate, half, solved = (s[name].at[step] for name in ("column", "other", "mate", "half", "solved"))
         here, away = z == step, z != step
         start, middle, end = gather(step, matrix, column, other, mate, *(s[name].at[step] for name in GATHER_FLAGS))
         start()
-        if step == 0:
-            for copy in loads:
-                copy.wait()
-
-            @pl.when(goes)
-            def _():
-                seeding.start()
+
+        @pl.when(first)
+        def _():
+            loads[1].wait()
+            loads[2].wait()
+            pl.when(goes)(seeding.start)
 
         middle()
-        if step == 3:
+
+        @pl.when(last)
+        def _():
             a_share[2]()
+
         end()
-        if step == 0:
-
-            @pl.when(goes)
-            def _():
-                seeding.wait_send()
-
-            @pl.when(comes)
-            def _():
-                seeding.wait_recv()
-
-            along_y(s["seed"], jnp.logical_and(holds, jnp.logical_not(stays)))[1]()
+
+        @pl.when(first)
+        def _():
+            pl.when(goes)(seeding.wait_send)
+            pl.when(comes)(seeding.wait_recv)
+            along_y(s["seed"], both_of(holds, jnp.logical_not(stays)))[1]()
             along_y(a_top, stays)[1]()
-        if step == 1:
+
+        @pl.when(second)
+        def _():
             for one in along_x(True):
                 one[1]()
 
         @pl.when(here)
         def _():
-            center(step, column, other, matrix, mate, half, *(s[name] for name in ("table", "fresh", "fresh_high", "fresh_low", "right_high", "right_low")))
-
-        if step == 0:
-            along_y(s["seed"], jnp.logical_and(holds, away))[2]()
-        if step == 1:
-            for one in along_x(away):
+            center(step, column, other, matrix, mate, half, *(s[name] for name in CENTER_SPACES))
+
+        @pl.when(both_of(first, away))
+        def _():
+            along_y(s["seed"], holds)[2]()
+
+        @pl.when(both_of(second, away))
+        def _():
+            for one in along_x(True):
                 one[2]()
-        if step == 2:
-
+
+        @pl.when(both_of(third, home))
+        def _():
+            a_center(s["strips"], a_top, c_top, s["a_solved"], *(s[name] for name in A_CENTER_SPACES))
+
+        @pl.when(last)
+        def _():
             @pl.when(home)
-            def _():
-                a_center(s["strips"], a_top, c_top, s["a_solved"], *(s[name] for name in ("a_table", "a_fresh", "a_fresh_high", "a_fresh_low", "a_right_high", "a_right_low")))
-
-        if step == 3:
-            @pl.when(jnp.logical_and(home, a_share[0] == 0))
             def _():
                 s["a_shared"][...] = s["a_solved"][...]
 
@@ -525,14 +560,16 @@
                 for h in range(CHUNKS):
                     a_give(h, s["a_solved"]).wait_recv()
 
-            pl.when(away)(finish_a)
-
         begin, relay, close = share(step, half, solved, *(s[name].at[step] for name in SHARE_FLAGS))
         begin()
+        pl.when(last)(finish_a)
         relay()
-        if step == 0:
-            along_y(s["seed"], jnp.logical_and(holds, here))[2]()
-            across = along_y(s["seed"], holds)
+
+        @pl.when(first)
+        def _():
+            @pl.when(here)
+            def _():
+                along_y(s["seed"], holds)[2]()
 
             @pl.when(stays)
             def _():
@@ -542,28 +579,31 @@
             def _():
                 s["strip"][...] = s["seed"][...]
 
-        if step == 1:
-            for one in along_x(here):
-                one[2]()
+            along_y(s["seed"], holds)[3]()
+
+        @pl.when(second)
+        def _():
+            @pl.when(here)
+            def _():
+                for one in along_x(True):
+                    one[2]()
+
             for at, one in enumerate(along_x(True)):
 
                 @pl.when(one[0] == 0)
                 def _():
                     s["strips"][at] = s["strip"][...]
 
-        if step == 3:
-            pl.when(here)(finish_a)
+                one[3]()
+
         close()
-        if step == 0:
-            across[3]()
-        if step == 1:
-            for one in along_x(True):
-                one[3]()
-        update(step, matrix, column, solved, s["matrix"].at[step], s["solved_high"], s["solved_low"])
-        matrix = s["matrix"].at[step]
-        if step == 2:
+        update(step, matrix, column, solved, s["matrix"].at[step + 1], s["solved_high"], s["solved_low"])
+
+        @pl.when(third)
+        def _():
             a_share[1]()
 
+    matrix = s["matrix"].at[STEPS_B // JOINED]
     lane = lax.broadcasted_iota(jnp.int32, (8, 128), 1)
     s["partial"][0] = jnp.where(lane == 0, squares(b[...]), squares(matrix[...]))
     s["partial"][1] = exchange(s["partial"].at[0], s["line"], s["line_sent"], s["line_got"], along)
@@ -582,6 +622,8 @@
 
 
 GATHER_FLAGS = ("y_sent", "y_got", "x_sent", "x_got", "far_sent", "far_got", "core_sent", "core_got")
+CENTER_SPACES = ("table", "fresh", "fresh_high", "fresh_low", "inverse_of", "right_high", "right_low")
+A_CENTER_SPACES = ("a_table", "a_fresh", "a_fresh_high", "a_fresh_low", "inverse_of", "a_right_high", "a_right_low")
 SHARE_FLAGS = ("z_sent", "z_got", "pass_sent", "pass_got")
 
 
@@ -599,9 +641,9 @@
     short = lambda *shape: pltpu.VMEM(shape, BF16)
     ringed = (2, CHUNKS)
     return dict(
-        a=full(*a_shape), c=full(*c_shape), load=flags(2),
+        a=full(*a_shape), c=full(*c_shape), load=flags(3), inverse_of=full(PANEL, PANEL),
         column=full(steps, 4, rows, cols), other=full(steps, 2, rows, cols), mate=full(steps, rows, cols),
-        half=full(steps, rows, cols), solved=full(steps, 2, rows, cols), matrix=full(steps, rows, cols),
+        half=full(steps, rows, cols), solved=full(steps, 2, rows, cols), matrix=full(steps + 1, rows, cols),
         table=full(order, order), fresh=full(PANEL, order), fresh_high=short(PANEL, order), fresh_low=short(PANEL, order),
         right_high=short(order, cols), right_low=short(order, cols), solved_high=short(order, cols), solved_low=short(order, cols),
         seed=full(*top), strip=full(*top), strips=full(2, *top), a_solved=full(a_order, wide), a_shared=full(a_order, wide),
@@ -628,7 +670,7 @@
     a_swept, c_swept, b_next = pl.pallas_call(
         whole_kernel,
         out_shape=[jax.ShapeDtypeStruct(shapes[at], F32) for at in (0, 2, 1)],
-        in_specs=[left, held, left],
+        in_specs=[left, left, left],
         out_specs=[left, left, held],
         scratch_shapes=list(spaces_of(*shapes).values()),
         compiler_params=pltpu.CompilerParams(vmem_limit_bytes=63 * 1024 * 1024, collective_id=0, has_side_effects=True),

time: 266 us -> 255 us (0.959)
  Pallas kernels: 261 us -> 249 us
    pallas_call x1, Pallas kernels: 261 us -> 249 us  [body(): pl.pallas_call(whole_kernel, out_shape=[jax.ShapeDtypeStruct(shapes[at],...]
where the time goes in v5:
time: 255 us
  Pallas kernels  249 us (98%)
  local copies, waits for them, and re-layouts  4.97 us (2%)
    pallas_call x1, Pallas kernels, body(): pl.pallas_call(whole_kernel, out_shape=[jax.ShapeDtypeStruct(shapes[at],...  249 us

profile of v5, /device:TPU:1, one launch (start us, length us, event | category | flops | bytes accessed | tf_op | source)
XLA Modules:
  0.0 255.0 jit_solution(17923068098867121001)
XLA Ops:
  0.6 249.4 %shard_map.58 = (f32[1024,512]{1,0:T(8,128)}, f32[1024,256]{1,0:T(8,128)}, f32[512,256]{1,0:T(8,128)}) custom-call(f32[1024,512]{1,0:T(8,128)} %a_hbm.1, f32[512,256]{1,0:T(8,128)} %b_hbm.1, f32[1024,256]{1,0:T(8,128)} %c_hbm.1), custom_call_target="tpu_custom_call" | custom-call | tf_op jit(solution)/shard_map/pallas_call | solution.py:670
  250.0 0.0 copy-start
  250.0 0.0 copy-start.1
  250.1 3.2 %copy.9 = f32[1024,512]{1,0:T(8,128)} copy(f32[1024,512]{1,0:T(8,128)} %get-tuple-element.6) | data formatting | bytes 4194304
  253.2 0.0 copy-done
  253.3 1.0 copy.10
  254.2 0.0 copy-done.1
  254.2 0.8 copy.11
Async XLA Ops:
  250.0 3.2 %copy-start = (f32[1024,256]{1,0:T(8,128)S(1)}, f32[1024,256]{1,0:T(8,128)}, u32[]{:S(2)}) copy-start(f32[1024,256]{1,0:T(8,128)} %get-tuple-element.7) | copy-start | bytes 3145732
  250.0 4.2 %copy-start.1 = (f32[512,256]{1,0:T(8,128)S(1)}, f32[512,256]{1,0:T(8,128)}, u32[]{:S(2)}) copy-start(f32[512,256]{1,0:T(8,128)} %get-tuple-element.8) | copy-start | bytes 1572868

commit v6 on v5

--- a/solution.py
+++ b/solution.py
@@ -56,7 +56,7 @@
     down = 1.0 / jnp.sqrt(jnp.sum(diagonal, axis=1, keepdims=True))
     across = 1.0 / jnp.sqrt(jnp.sum(diagonal, axis=0, keepdims=True))
     scaled = pivot * down * across
-    ceiling = jnp.max(jnp.sum(jnp.abs(scaled), axis=1, keepdims=True), axis=0, keepdims=True)
+    ceiling = jnp.max(jnp.sum(jnp.abs(scaled), axis=0, keepdims=True), axis=1, keepdims=True)
     eye = jnp.where(unit, 1.0, 0.0)
     power = eye - scaled / ceiling
     fill()
@@ -249,7 +249,7 @@
     return left if right is True else jnp.logical_and(left, right)
 
 
-def spread(axis, step, source, landing, sent, received, follow, active=True):
+def spread(axis, step, source, landing, sent, received, follow, active=True, around=()):
     place = lax.axis_index(axis)
     apart = lax.rem(place - step + 4, 4)
     up, down = {axis: ring(place, 1)}, {axis: ring(place, 3)}
@@ -261,7 +261,8 @@
         @pl.when(both(apart == 0, active))
         def _():
             for one, two in zip(AHEAD + BEHIND, BEHIND + AHEAD):
-                copy(source, one, 0).start()
+                if one not in around:
+                    copy(source, one, 0).start()
                 copy(source, two, 1).start()
             for h in range(CHUNKS):
                 follow(h, source)
@@ -276,7 +277,7 @@
 
         @pl.when(both(apart == 1, active))
         def _():
-            take(AHEAD + BEHIND, AHEAD, 0)
+            take([h for h in AHEAD + BEHIND if h not in around] + list(around), AHEAD, 0)
 
         @pl.when(both(apart == 3, active))
         def _():
@@ -284,13 +285,14 @@
 
         @pl.when(both(apart == 2, active))
         def _():
-            take([h for two in zip(AHEAD, BEHIND) for h in two], (), 0)
+            take([h for two in zip(AHEAD, BEHIND) for h in two], around, 1)
 
     def finish():
         @pl.when(both(apart == 0, active))
         def _():
             for h in range(CHUNKS):
-                copy(source, h, 0).wait_send()
+                if h not in around:
+                    copy(source, h, 0).wait_send()
                 copy(source, h, 1).wait_send()
 
         @pl.when(both(apart == 1, active))
@@ -302,6 +304,13 @@
         def _():
             for h in BEHIND:
                 copy(landing, h, 1).wait_send()
+
+        if around:
+
+            @pl.when(both(apart == 2, active))
+            def _():
+                for h in around:
+                    copy(landing, h, 1).wait_send()
 
     return apart, begin, relay, finish
 
@@ -379,6 +388,13 @@
         maybe_give(far, column.at[far])
 
     def end():
+        @pl.when(centered)
+        def _():
+            swap.wait_recv()
+            give(0, matrix).wait_recv()
+            give(1, matrix).wait_recv()
+
+    def drain():
         finish()
         for h in range(CHUNKS):
             for copy in sideways(h, matrix):
@@ -387,11 +403,11 @@
 
         @pl.when(centered)
         def _():
-            swap.wait()
-            give(0, matrix).wait()
-            give(1, matrix).wait()
-
-    return start, middle, end
+            swap.wait_send()
+            give(0, matrix).wait_send()
+            give(1, matrix).wait_send()
+
+    return start, middle, end, drain
 
 
 def share(step, half, solved, z_sent, z_got, core_sent, core_got):
@@ -404,20 +420,23 @@
     def follow(h, ref):
         give(h, ref).start()
 
-    apart, begin, relay, finish = spread("z", step, half, solved.at[core], z_sent, z_got, follow)
+    apart, begin, relay, finish = spread("z", step, half, solved.at[core], z_sent, z_got, follow, around=BEHIND[:2])
 
     def end():
         @pl.when(apart == 0)
         def _():
             solved[core] = half[...]
 
+        for h in range(CHUNKS):
+            ref = solved.at[1 - core, chunk(h)]
+            send(ref, ref, core_sent.at[h], core_got.at[h], partner).wait_recv()
+
+    def drain():
         finish()
         for h in range(CHUNKS):
             give(h, half).wait_send()
-            ref = solved.at[1 - core, chunk(h)]
-            send(ref, ref, core_sent.at[h], core_got.at[h], partner).wait_recv()
-
-    return begin, relay, end
+
+    return begin, relay, end, drain
 
 
 def peers():
@@ -503,7 +522,7 @@
         matrix = s["matrix"].at[step]
         column, other, mate, half, solved = (s[name].at[step] for name in ("column", "other", "mate", "half", "solved"))
         here, away = z == step, z != step
-        start, middle, end = gather(step, matrix, column, other, mate, *(s[name].at[step] for name in GATHER_FLAGS))
+        start, middle, end, gathered = gather(step, matrix, column, other, mate, *(s[name].at[step] for name in GATHER_FLAGS))
         start()
 
         @pl.when(first)
@@ -560,7 +579,7 @@
                 for h in range(CHUNKS):
                     a_give(h, s["a_solved"]).wait_recv()
 
-        begin, relay, close = share(step, half, solved, *(s[name].at[step] for name in SHARE_FLAGS))
+        begin, relay, close, shared = share(step, half, solved, *(s[name].at[step] for name in SHARE_FLAGS))
         begin()
         pl.when(last)(finish_a)
         relay()
@@ -578,8 +597,6 @@
             @pl.when(comes)
             def _():
                 s["strip"][...] = s["seed"][...]
-
-            along_y(s["seed"], holds)[3]()
 
         @pl.when(second)
         def _():
@@ -594,10 +611,19 @@
                 def _():
                     s["strips"][at] = s["strip"][...]
 
-                one[3]()
-
         close()
         update(step, matrix, column, solved, s["matrix"].at[step + 1], s["solved_high"], s["solved_low"])
+        gathered()
+        shared()
+
+        @pl.when(first)
+        def _():
+            along_y(s["seed"], holds)[3]()
+
+        @pl.when(second)
+        def _():
+            for one in along_x(True):
+                one[3]()
 
         @pl.when(third)
         def _():

time: 255 us -> 253 us (level)
  no operation moved by 1% of the time
where the time goes in v6:
time: 253 us
  Pallas kernels  248 us (98%)
  local copies, waits for them, and re-layouts  4.97 us (2%)
    pallas_call x1, Pallas kernels, body(): pl.pallas_call(whole_kernel, out_shape=[jax.ShapeDtypeStruct(shapes[at],...  248 us

profile of v6, /device:TPU:1, one launch (start us, length us, event | category | flops | bytes accessed | tf_op | source)
XLA Modules:
  0.0 253.2 jit_solution(2125833291993579378)
XLA Ops:
  0.6 247.6 %shard_map.58 = (f32[1024,512]{1,0:T(8,128)}, f32[1024,256]{1,0:T(8,128)}, f32[512,256]{1,0:T(8,128)}) custom-call(f32[1024,512]{1,0:T(8,128)} %a_hbm.1, f32[512,256]{1,0:T(8,128)} %b_hbm.1, f32[1024,256]{1,0:T(8,128)} %c_hbm.1), custom_call_target="tpu_custom_call" | custom-call | tf_op jit(solution)/shard_map/pallas_call | solution.py:696
  248.3 0.0 copy-start
  248.3 0.0 copy-start.1
  248.3 3.2 %copy.9 = f32[1024,512]{1,0:T(8,128)} copy(f32[1024,512]{1,0:T(8,128)} %get-tuple-element.6) | data formatting | bytes 4194304
  251.5 0.0 copy-done
  251.5 1.0 copy.10
  252.4 0.0 copy-done.1
  252.5 0.8 copy.11
Async XLA Ops:
  248.3 3.2 %copy-start = (f32[1024,256]{1,0:T(8,128)S(1)}, f32[1024,256]{1,0:T(8,128)}, u32[]{:S(2)}) copy-start(f32[1024,256]{1,0:T(8,128)} %get-tuple-element.7) | copy-start | bytes 3145732
  248.3 4.2 %copy-start.1 = (f32[512,256]{1,0:T(8,128)S(1)}, f32[512,256]{1,0:T(8,128)}, u32[]{:S(2)}) copy-start(f32[512,256]{1,0:T(8,128)} %get-tuple-element.8) | copy-start | bytes 1572868

commit v7 on v6

--- a/solution.py
+++ b/solution.py
@@ -383,9 +383,12 @@
             arrive(left, two, x_got.at[0, two])
         maybe_give(left, column.at[left])
         maybe_give(right, column.at[right])
-        for h in range(CHUNKS):
+        slot = lax.rem(far, 2)
+        ours = jnp.logical_and(centered, far // 2 == core)
+        for h in [h for two in zip(AHEAD, BEHIND) for h in two]:
             arrive(far, h, far_got.at[h])
-        maybe_give(far, column.at[far])
+            late = send(column.at[far, chunk(h)], other.at[slot, chunk(h)], core_sent.at[slot], core_got.at[slot], partner)
+            pl.when(ours)(late.start)
 
     def end():
         @pl.when(centered)
@@ -420,7 +423,7 @@
     def follow(h, ref):
         give(h, ref).start()
 
-    apart, begin, relay, finish = spread("z", step, half, solved.at[core], z_sent, z_got, follow, around=BEHIND[:2])
+    apart, begin, relay, finish = spread("z", step, half, solved.at[core], z_sent, z_got, follow, around=BEHIND[:1])
 
     def end():
         @pl.when(apart == 0)

time: 253 us -> 251 us (level)
  Pallas kernels: 248 us -> 245 us
    pallas_call x1, Pallas kernels: 248 us -> 245 us  [body(): pl.pallas_call(whole_kernel, out_shape=[jax.ShapeDtypeStruct(shapes[at],...]
where the time goes in v7:
time: 251 us
  Pallas kernels  245 us (98%)
  local copies, waits for them, and re-layouts  4.97 us (2%)
    pallas_call x1, Pallas kernels, body(): pl.pallas_call(whole_kernel, out_shape=[jax.ShapeDtypeStruct(shapes[at],...  245 us

profile of v7, /device:TPU:1, one launch (start us, length us, event | category | flops | bytes accessed | tf_op | source)
XLA Modules:
  0.0 250.6 jit_solution(11684938702592919799)
XLA Ops:
  0.6 244.9 %shard_map.58 = (f32[1024,512]{1,0:T(8,128)}, f32[1024,256]{1,0:T(8,128)}, f32[512,256]{1,0:T(8,128)}) custom-call(f32[1024,512]{1,0:T(8,128)} %a_hbm.1, f32[512,256]{1,0:T(8,128)} %b_hbm.1, f32[1024,256]{1,0:T(8,128)} %c_hbm.1), custom_call_target="tpu_custom_call" | custom-call | tf_op jit(solution)/shard_map/pallas_call | solution.py:699
  245.6 0.0 copy-start
  245.6 0.0 copy-start.1
  245.6 3.2 %copy.9 = f32[1024,512]{1,0:T(8,128)} copy(f32[1024,512]{1,0:T(8,128)} %get-tuple-element.6) | data formatting | bytes 4194304
  248.8 0.0 copy-done
  248.8 1.0 copy.10
  249.8 0.0 copy-done.1
  249.8 0.8 copy.11
Async XLA Ops:
  245.6 3.2 %copy-start = (f32[1024,256]{1,0:T(8,128)S(1)}, f32[1024,256]{1,0:T(8,128)}, u32[]{:S(2)}) copy-start(f32[1024,256]{1,0:T(8,128)} %get-tuple-element.7) | copy-start | bytes 3145732
  245.6 4.2 %copy-start.1 = (f32[512,256]{1,0:T(8,128)S(1)}, f32[512,256]{1,0:T(8,128)}, u32[]{:S(2)}) copy-start(f32[512,256]{1,0:T(8,128)} %get-tuple-element.8) | copy-start | bytes 1572868

commit v8 on v7

--- a/solution.py
+++ b/solution.py
@@ -150,8 +150,8 @@
 
         @pl.when(core == at)
         def _():
-            for q in range(JOINED):
-                table[pair[at], q * PANEL : (q + 1) * PANEL] = mine[q]
+            far = ring(lax.axis_index("x"), 2)
+            table[pair[at], pl.ds(pl.multiple_of(far * PANEL, PANEL), PANEL)] = mine[far]
             for q in range(2):
                 across = 2 * (1 - at) + q
                 table[pair[1 - at], across * PANEL : (across + 1) * PANEL] = other[q]
@@ -319,7 +319,7 @@
     pass
 
 
-def gather(step, matrix, column, other, mate, y_sent, y_got, x_sent, x_got, far_sent, far_got, core_sent, core_got):
+def gather(early, step, matrix, column, other, mate, y_sent, y_got, x_sent, x_got, far_sent, far_got, core_sent, core_got):
     x = lax.axis_index("x")
     core = lax.axis_index("core")
     right, left, far = ring(x, 1), ring(x, 3), ring(x, 2)
@@ -383,6 +383,8 @@
             arrive(left, two, x_got.at[0, two])
         maybe_give(left, column.at[left])
         maybe_give(right, column.at[right])
+        for place in (x, left, right):
+            early(place)
         slot = lax.rem(far, 2)
         ours = jnp.logical_and(centered, far // 2 == core)
         for h in [h for two in zip(AHEAD, BEHIND) for h in two]:
@@ -525,7 +527,14 @@
         matrix = s["matrix"].at[step]
         column, other, mate, half, solved = (s[name].at[step] for name in ("column", "other", "mate", "half", "solved"))
         here, away = z == step, z != step
-        start, middle, end, gathered = gather(step, matrix, column, other, mate, *(s[name].at[step] for name in GATHER_FLAGS))
+
+        def early(place):
+            @pl.when(here)
+            def _():
+                rows = pl.ds(pl.multiple_of(core * matrix.shape[0], PANEL), matrix.shape[0])
+                s["table"][rows, pl.ds(pl.multiple_of(place * PANEL, PANEL), PANEL)] = column[place]
+
+        start, middle, end, gathered = gather(early, step, matrix, column, other, mate, *(s[name].at[step] for name in GATHER_FLAGS))
         start()
 
         @pl.when(first)

time: 251 us -> 250 us (level)
  no operation moved by 1% of the time
where the time goes in v8:
time: 250 us
  Pallas kernels  245 us (98%)
  local copies, waits for them, and re-layouts  4.97 us (2%)
    pallas_call x1, Pallas kernels, body(): pl.pallas_call(whole_kernel, out_shape=[jax.ShapeDtypeStruct(shapes[at],...  245 us

profile of v8, /device:TPU:1, one launch (start us, length us, event | category | flops | bytes accessed | tf_op | source)
XLA Modules:
  0.0 250.3 jit_solution(15741917772816975333)
XLA Ops:
  0.6 244.6 %shard_map.58 = (f32[1024,512]{1,0:T(8,128)}, f32[1024,256]{1,0:T(8,128)}, f32[512,256]{1,0:T(8,128)}) custom-call(f32[1024,512]{1,0:T(8,128)} %a_hbm.1, f32[512,256]{1,0:T(8,128)} %b_hbm.1, f32[1024,256]{1,0:T(8,128)} %c_hbm.1), custom_call_target="tpu_custom_call" | custom-call | tf_op jit(solution)/shard_map/pallas_call | solution.py:708
  245.3 0.0 copy-start
  245.3 0.0 copy-start.1
  245.3 3.2 %copy.9 = f32[1024,512]{1,0:T(8,128)} copy(f32[1024,512]{1,0:T(8,128)} %get-tuple-element.6) | data formatting | bytes 4194304
  248.5 0.0 copy-done
  248.5 1.0 copy.10
  249.5 0.0 copy-done.1
  249.5 0.8 copy.11
Async XLA Ops:
  245.3 3.2 %copy-start = (f32[1024,256]{1,0:T(8,128)S(1)}, f32[1024,256]{1,0:T(8,128)}, u32[]{:S(2)}) copy-start(f32[1024,256]{1,0:T(8,128)} %get-tuple-element.7) | copy-start | bytes 3145732
  245.3 4.2 %copy-start.1 = (f32[512,256]{1,0:T(8,128)S(1)}, f32[512,256]{1,0:T(8,128)}, u32[]{:S(2)}) copy-start(f32[512,256]{1,0:T(8,128)} %get-tuple-element.8) | copy-start | bytes 1572868
